TPU v7x, 256 devices: a whole 4x4x8 slice. The times are simulated.
256 devices in a mesh: seq: 32 (over z, x), head: 8 (over y, core).
Axes of the slice: x: 4, y: 4, z: 8, core: 2. Of those that a mesh axis runs over, the one named last changes fastest.
Arguments:
- queries: bfloat16 [8192, 1024], P('seq', 'head'), may hold values from -16 to 16
- keys: bfloat16 [8192, 1024], P(('seq', 'head')), may hold values from -16 to 16
- values: bfloat16 [8192, 1024], P(('seq', 'head')), may hold values from -6 to 6
- out_grad: bfloat16 [8192, 1024], P('seq', 'head'), may hold values from -6 to 6
Outputs:
- attended: bfloat16 [8192, 1024], P('seq', 'head')
- query_grad: float32 [8192, 1024], P('seq', 'head')
- key_grad: float32 [8192, 1024], P('seq', 'head')
- value_grad: float32 [8192, 1024], P('seq', 'head')
All inputs are finite; a program needn't handle non-finite values.
Results may differ from a plain program's by a relative error of at most 0.0095.
Values may be sent and summed in bfloat16 or wider, within the bound.
No kernel may reach another device: no remote copies, remote signals or barrier semaphores. Data moves between devices by JAX's collectives and lax.ppermute only.
A program may use at most 64 MiB of HBM per device.

v0:
```python
import math

import jax
import jax.numpy as jnp
from jax import lax
from jax.sharding import Mesh
from jax.sharding import PartitionSpec as P

SEQ = ("seq_0", "seq_1")
SEQ_HEAD = ("seq_0", "seq_1", "head")


masked_value = -1e30


def whole_of(array, axes, dim):
    filled = array
    for number in range(len(axes) - 1, -1, -1):
        filled = lax.all_gather(filled, axes[number], axis=dim, tiled=True)
    return filled


def joined_along(parts, dim):
    dims = list(parts.shape[1:])
    dims[dim] *= parts.shape[0]
    return jnp.moveaxis(parts, 0, dim).reshape(dims)


def gather_packed(arrays, axis, dims):
    ravelled = jnp.concatenate([a.reshape(-1) for a in arrays])
    lines, at, gathered = (lax.all_gather(ravelled, axis), 0, [])
    for a, dim in zip(arrays, dims):
        parts = lines[:, at : at + a.size].reshape(-1, *a.shape)
        gathered.append(joined_along(parts, dim))
        at += a.size
    return tuple(gathered)


def key_block(length, row_count):
    return min(length, max(1024, 2 * row_count))


def attend_range(queries, qstart, whole_keys, whole_values, key_low, key_high, scaling):
    row_count, head_width = queries.shape
    length = whole_keys.shape[0]
    span_rows = key_block(length, row_count)
    query_pos = qstart + jnp.arange(row_count, dtype=jnp.int32)

    def attend_compute(running, kstart):
        weighted, rowmax, rowsum = running
        key_piece = lax.dynamic_slice_in_dim(whole_keys, kstart, span_rows, 0)
        value_piece = lax.dynamic_slice_in_dim(whole_values, kstart, span_rows, 0)
        key_pos = kstart + jnp.arange(span_rows, dtype=jnp.int32)
        allowed = (
            (key_pos[None, :] <= query_pos[:, None])
            & (key_pos[None, :] >= key_low)
            & (key_pos[None, :] < key_high)
        )
        scores = (
            jnp.einsum("qd,kd->qk", queries, key_piece, preferred_element_type=jnp.float32)
            * scaling
        )
        scores = jnp.where(allowed, scores, masked_value)
        new_max = jnp.maximum(rowmax, jnp.max(scores, axis=1))
        weights = jnp.where(allowed, jnp.exp(scores - new_max[:, None]), 0.0)
        factor = jnp.exp(rowmax - new_max)
        rowsum = rowsum * factor + jnp.sum(weights, axis=1)
        weighted = weighted * factor[:, None] + jnp.dot(
            weights.astype(jnp.bfloat16), value_piece, preferred_element_type=jnp.float32
        )
        return (weighted, new_max, rowsum)

    def attend_advance(counter, running):
        kstart = counter * span_rows
        needed = (
            (kstart < key_high) & (kstart + span_rows > key_low) & (kstart < qstart + row_count)
        )
        return lax.cond(
            needed,
            lambda previous: attend_compute(previous, kstart),
            lambda previous: previous,
            running,
        )

    initial = (
        jnp.zeros((row_count, head_width), jnp.float32),
        jnp.full((row_count,), masked_value, jnp.float32),
        jnp.zeros((row_count,), jnp.float32),
    )
    return lax.fori_loop(0, length // span_rows, attend_advance, initial)


def backward_range(
    queries,
    out_grad,
    log_norm,
    row_delta,
    qstart,
    whole_keys,
    whole_values,
    key_low,
    key_high,
    scaling,
):
    row_count, head_width = queries.shape
    length = whole_keys.shape[0]
    span_rows = key_block(length, row_count)
    query_pos = qstart + jnp.arange(row_count, dtype=jnp.int32)

    def backward_compute(running, kstart):
        query_part, terms = running
        key_piece = lax.dynamic_slice_in_dim(whole_keys, kstart, span_rows, 0)
        value_piece = lax.dynamic_slice_in_dim(whole_values, kstart, span_rows, 0)
        key_pos = kstart + jnp.arange(span_rows, dtype=jnp.int32)
        allowed = (
            (key_pos[None, :] <= query_pos[:, None])
            & (key_pos[None, :] >= key_low)
            & (key_pos[None, :] < key_high)
        )
        scores = (
            jnp.einsum("qd,kd->qk", queries, key_piece, preferred_element_type=jnp.float32)
            * scaling
        )
        probs = jnp.where(allowed, jnp.exp(scores - log_norm[:, None]), 0.0)
        grad_probs = jnp.einsum(
            "qd,kd->qk", out_grad, value_piece, preferred_element_type=jnp.float32
        )
        grad_scores = (probs * (grad_probs - row_delta[:, None]) * scaling).astype(jnp.bfloat16)
        query_part = query_part + jnp.dot(
            grad_scores, key_piece, preferred_element_type=jnp.float32
        )
        return (query_part, terms)

    def backward_advance(counter, running):
        kstart = counter * span_rows
        needed = (
            (kstart < key_high) & (kstart + span_rows > key_low) & (kstart < qstart + row_count)
        )
        return lax.cond(
            needed,
            lambda previous: backward_compute(previous, kstart),
            lambda previous: previous,
            running,
        )

    initial = (jnp.zeros((row_count, head_width), jnp.float32), None)
    return lax.fori_loop(0, length // span_rows, backward_advance, initial)


def key_range(all_rows, all_grads, all_norms, all_deltas, own_keys, own_values, kstart, scaling):
    length = all_rows.shape[0]
    row_count, head_width = own_keys.shape
    span_rows = key_block(length, row_count)
    key_pos = kstart + jnp.arange(row_count, dtype=jnp.int32)

    def key_compute(running, qstart):
        key_total, value_total = running
        query_piece = lax.dynamic_slice_in_dim(all_rows, qstart, span_rows, 0)
        grad_piece = lax.dynamic_slice_in_dim(all_grads, qstart, span_rows, 0)
        norm_piece = lax.dynamic_slice_in_dim(all_norms, qstart, span_rows, 0)
        delta_piece = lax.dynamic_slice_in_dim(all_deltas, qstart, span_rows, 0)
        query_pos = qstart + jnp.arange(span_rows, dtype=jnp.int32)
        allowed = key_pos[None, :] <= query_pos[:, None]
        scores = (
            jnp.einsum("qd,kd->qk", query_piece, own_keys, preferred_element_type=jnp.float32)
            * scaling
        )
        probs = jnp.where(allowed, jnp.exp(scores - norm_piece[:, None]), 0.0)
        grad_probs = jnp.einsum(
            "qd,kd->qk", grad_piece, own_values, preferred_element_type=jnp.float32
        )
        grad_scores = (probs * (grad_probs - delta_piece[:, None]) * scaling).astype(jnp.bfloat16)
        key_total = key_total + jnp.einsum(
            "qk,qd->kd", grad_scores, query_piece, preferred_element_type=jnp.float32
        )
        value_total = value_total + jnp.einsum(
            "qk,qd->kd", probs.astype(jnp.bfloat16), grad_piece, preferred_element_type=jnp.float32
        )
        return (key_total, value_total)

    def key_advance(counter, running):
        qstart = counter * span_rows
        needed = qstart + span_rows > kstart
        return lax.cond(
            needed,
            lambda previous: key_compute(previous, qstart),
            lambda previous: previous,
            running,
        )

    initial = (
        jnp.zeros((row_count, head_width), jnp.float32),
        jnp.zeros((row_count, head_width), jnp.float32),
    )
    return lax.fori_loop(0, length // span_rows, key_advance, initial)


def per_device(queries, keys, values, out_grad):
    row_count, head_width = queries.shape
    scaling = 1.0 / math.sqrt(head_width)
    local_keys, local_values = (
        lax.all_to_all(keys, "head", split_axis=1, concat_axis=0, tiled=True),
        lax.all_to_all(values, "head", split_axis=1, concat_axis=0, tiled=True),
    )
    whole_keys, whole_values = (whole_of(local_keys, SEQ, 0), whole_of(local_values, SEQ, 0))
    length = whole_keys.shape[0]
    device = lax.axis_index(SEQ)
    qstart = device * row_count
    weighted, rowmax, rowsum = attend_range(
        queries, qstart, whole_keys, whole_values, 0, length, scaling
    )
    output = weighted / rowsum[:, None]
    log_norm = rowmax + jnp.log(rowsum)
    attended = output.astype(jnp.bfloat16)
    row_delta = jnp.sum(out_grad.astype(jnp.float32) * output, axis=1)
    query_grad, unused = backward_range(
        queries, out_grad, log_norm, row_delta, qstart, whole_keys, whole_values, 0, length, scaling
    )
    all_rows, all_grads = (whole_of(queries, SEQ, 0), whole_of(out_grad, SEQ, 0))
    all_norms, all_deltas = gather_packed((log_norm, row_delta), SEQ, (0, 0))
    key_grad, value_grad = key_range(
        all_rows, all_grads, all_norms, all_deltas, local_keys, local_values, qstart, scaling
    )
    return (attended, query_grad, key_grad, value_grad)


def solution(mesh):
    split = Mesh(mesh.devices.reshape(8, 4, mesh.shape["head"]), ("seq_0", "seq_1", "head"))
    return jax.shard_map(
        per_device,
        mesh=split,
        in_specs=(P(SEQ, "head"), P(SEQ_HEAD, None), P(SEQ_HEAD, None), P(SEQ, "head")),
        out_specs=(P(SEQ, "head"), P(SEQ, "head"), P(SEQ, "head"), P(SEQ, "head")),
        check_vma=False,
    )
```

profile of v0, /device:TPU:8, one launch (start us, length us, event | category | flops | bytes accessed | tf_op | source)
XLA Modules:
  0.0 247.4 jit_solution(4875026922688107261)
XLA Ops:
  7.2 0.0 all-gather.7.cloned.1.call-start
  7.2 0.8 copy-done
  8.0 8.9 %all_to_all.38 = bf16[32,8,128]{2,0,1:T(8,128)(2,1)S(1)} all-to-all(bf16[32,8,128]{2,0,1:T(8,128)(2,1)S(1)} %copy_bitcast_fusion.1), channel_id=1, replica_groups=mesh['seq_0'=8,'seq_1'=4,'head'=8] {'head'}, dimensions={1} | all-to-all | bytes 131072 | tf_op jit(solution)/shard_map/all_to_all | solution.py:202
  16.9 13.3 %all_gather.30 = bf16[1024,128]{1,0:T(8,128)(2,1)} all-gather(bf16[256,128]{1,0:T(8,128)(2,1)S(1)} %bitcast.53), channel_id=1, replica_groups=mesh['seq_0'=8,'seq_1'=4,'head'=8] {'seq_1'}, dimensions={0}, use_global_device_ids=true | all-gather | bytes 327680 | tf_op jit(solution)/shard_map/all_gather | solution.py:19
  30.3 0.0 all-gather.9.cloned.1.call-start
  30.3 0.9 copy_bitcast_fusion
  31.2 8.0 %all_to_all.39 = bf16[32,8,128]{2,0,1:T(8,128)(2,1)S(1)} all-to-all(bf16[32,8,128]{2,0,1:T(8,128)(2,1)S(1)} %copy_bitcast_fusion), channel_id=1, replica_groups=mesh['seq_0'=8,'seq_1'=4,'head'=8] {'head'}, dimensions={1} | all-to-all | bytes 131072 | tf_op jit(solution)/shard_map/all_to_all | solution.py:203
  39.2 13.0 %all_gather.32 = bf16[1024,128]{1,0:T(8,128)(2,1)} all-gather(bf16[256,128]{1,0:T(8,128)(2,1)S(1)} %bitcast.51), channel_id=1, replica_groups=mesh['seq_0'=8,'seq_1'=4,'head'=8] {'seq_1'}, dimensions={0}, use_global_device_ids=true | all-gather | bytes 327680 | tf_op jit(solution)/shard_map/all_gather | solution.py:19
  52.2 0.0 all-gather.9.cloned.1.call-update
  52.2 0.0 all-gather.11.cloned.1.call-start
  52.2 14.0 %all_gather.34 = bf16[1024,128]{1,0:T(8,128)(2,1)} all-gather(bf16[256,128]{1,0:T(8,128)(2,1)} %param.16), channel_id=1, replica_groups=mesh['seq_0'=8,'seq_1'=4,'head'=8] {'seq_1'}, dimensions={0}, use_global_device_ids=true | all-gather | bytes 327680 | tf_op jit(solution)/shard_map/all_gather | solution.py:19
  66.3 0.0 all-gather.13.cloned.1.call-start
  66.4 13.1 %all_gather.38 = bf16[1024,128]{1,0:T(8,128)(2,1)} all-gather(bf16[256,128]{1,0:T(8,128)(2,1)S(1)} %copy-done.4), channel_id=1, replica_groups=mesh['seq_0'=8,'seq_1'=4,'head'=8] {'seq_1'}, dimensions={0}, use_global_device_ids=true | all-gather | bytes 327680 | tf_op jit(solution)/shard_map/all_gather | solution.py:19
  79.5 0.0 all-gather.13.cloned.1.call-update
  79.5 0.0 all-gather.7.cloned.1.call-done
  79.5 34.4 %all-gather.9.cloned.1.call-done = bf16[8192,128]{1,0:T(8,128)(2,1)} async-done(((bf16[1024,128]{1,0:T(8,128)(2,1)}), bf16[8192,128]{1,0:T(8,128)(2,1)}) %all-gather.9.cloned.1.call-update) | async-done | bytes 2097168 | tf_op jit(solution)/shard_map/all_gather | solution.py:19
  113.9 5.1 %while.56 = (s32[]{:T(128)}, f32[256,128]{1,0:T(8,128)S(1)}, f32[256]{0:T(256)S(1)}, f32[256]{0:T(256)S(1)}, s32[]{:T(128)}, /*index=5*/bf16[8192,128]{1,0:T(8,1...) while((s32[]{:T(128)}, f32[256,128]{1,0:T(8,128)S(1)}, ...), condition=%wide.region_5.6_spmd.clone, body=%wide.region_0.5_spmd.clone.sunk | while | flops 139006736 | bytes 4045177 | solution.py:90
  114.0 4.6 %conditional.10 = ((f32[256,128]{1,0:T(8,128)S(1)}, f32[256]{0:T(256)S(1)}, f32[256]{0:T(256)S(1)})) conditional(s32[]{:T(128)} %convert_element_type.68, (f32[256,128]{1,0:T(8,128)S(1)}, f32[256]{0:T(256)S(1)}, f32[256]{0:T(256)S(1)}) %tuple.146, (s32[]{:T(128)}, s32[]{:T(128)}, bf16[8192,128]{1,0:T(8,128)(2,1)}, bf16[256,128]{1,0:T(8,128)(2,1)S(1)}, ...), branch_computations={%region_1.0_spmd, %region_2.4_spmd} | conditional | flops 139006720 | bytes 4043862 | solution.py:78
  114.1 1.9 fusion.68
  115.9 0.8 fusion.8
  116.8 1.8 convolution_add_fusion
  119.1 0.7 multiply_reduce_fusion
  119.8 80.2 %all-gather.1 = f32[32,1,512]{2,1,0:T(1,128)S(1)} all-gather(f32[1,1,512]{2,1,0:T(1,128)S(1)} %bitcast.58), channel_id=2, replica_groups=mesh['seq_0'=8,'seq_1'=4,'head'=8] {'seq_0','seq_1'}, dimensions={0}, use_global_device_ids=true | all-gather | bytes 67584 | tf_op jit(solution)/shard_map/all_gather | solution.py:31
  200.1 3.5 %while.57 = (s32[]{:T(128)}, f32[256,128]{1,0:T(8,128)S(1)}, s32[]{:T(128)}, bf16[8192,128]{1,0:T(8,128)(2,1)}, bf16[256,128]{1,0:T(8,128)(2,1)S(1)}, /*index=5*...) while((s32[]{:T(128)}, f32[256,128]{1,0:T(8,128)S(1)}, ...), condition=%wide.region_10.11_spmd.clone, body=%wide.region_7.10_spmd.clone.sunk | while | flops 203985168 | bytes 3296597 | solution.py:147
  200.2 3.0 %conditional.11 = (f32[256,128]{1,0:T(8,128)S(1)}) conditional(s32[]{:T(128)} %convert_element_type.69, f32[256,128]{1,0:T(8,128)S(1)} %get-tuple-element.1194, (s32[]{:T(128)}, s32[]{:T(128)}, bf16[8192,128]{1,0:T(8,128)(2,1)}, bf16[256,128]{1,0:T(8,128)(2,1)S(1)}, f32[256]{0:T(256)S(1)}, /*index=5*/bf16[8192,128]{1,0:T(8,128)(2,1)}, ...), branch_computations={%region_8.8_spmd, %region_9.9_spmd} | conditional | flops 203985152 | bytes 3295290 | solution.py:139
  200.2 1.4 fusion.30
  201.7 1.5 fusion.33
  203.6 0.0 all-gather.11.cloned.1.call-done
  203.7 0.6 copy-done.3
  204.3 35.9 %while.58 = (s32[]{:T(128)}, f32[256,128]{1,0:T(8,128)S(1)}, f32[256,128]{1,0:T(8,128)S(1)}, s32[]{:T(128)}, bf16[8192,128]{1,0:T(8,128)(2,1)}, /*index=5*/bf16[...) while((s32[]{:T(128)}, f32[256,128]{1,0:T(8,128)S(1)}, ...), condition=%wide.region_14.15_spmd.clone.clone, body=%wide.region_11.14_spmd.clone.clone.sunk | while | flops 270861568 | bytes 4887901 | solution.py:195
  204.3 4.4 %conditional.12 = ((f32[256,128]{1,0:T(8,128)S(1)}, f32[256,128]{1,0:T(8,128)S(1)})) conditional(s32[]{:T(128)} %convert_element_type.70, (f32[256,128]{1,0:T(8,128)S(1)}, f32[256,128]{1,0:T(8,128)S(1)}) %tuple.151, (s32[]{:T(128)}, s32[]{:T(128)}, bf16[8192,128]{1,0:T(8,128)(2,1)}, bf16[256,128]{1,0:T(8,128)(2,1)S(1)}, f32[8192]{0:T(1024)S(1)}, ...), branch_computations={%region_12.12_spmd, %region_13.13_spmd} | conditional | flops 270861568 | bytes 4886610 | solution.py:184
  204.3 1.4 fusion.50
  205.7 1.7 fusion.53
  207.4 1.3 convolution_add_fusion.1
  208.7 4.5 %conditional.12 = ((f32[256,128]{1,0:T(8,128)S(1)}, f32[256,128]{1,0:T(8,128)S(1)})) conditional(s32[]{:T(128)} %convert_element_type.70, (f32[256,128]{1,0:T(8,128)S(1)}, f32[256,128]{1,0:T(8,128)S(1)}) %tuple.151, (s32[]{:T(128)}, s32[]{:T(128)}, bf16[8192,128]{1,0:T(8,128)(2,1)}, bf16[256,128]{1,0:T(8,128)(2,1)S(1)}, f32[8192]{0:T(1024)S(1)}, ...), branch_computations={%region_12.12_spmd, %region_13.13_spmd} | conditional | flops 270861568 | bytes 4886610 | solution.py:184
  208.8 1.4 fusion.50
  210.2 1.7 fusion.53
  211.9 1.3 convolution_add_fusion.1
  213.2 4.5 %conditional.12 = ((f32[256,128]{1,0:T(8,128)S(1)}, f32[256,128]{1,0:T(8,128)S(1)})) conditional(s32[]{:T(128)} %convert_element_type.70, (f32[256,128]{1,0:T(8,128)S(1)}, f32[256,128]{1,0:T(8,128)S(1)}) %tuple.151, (s32[]{:T(128)}, s32[]{:T(128)}, bf16[8192,128]{1,0:T(8,128)(2,1)}, bf16[256,128]{1,0:T(8,128)(2,1)S(1)}, f32[8192]{0:T(1024)S(1)}, ...), branch_computations={%region_12.12_spmd, %region_13.13_spmd} | conditional | flops 270861568 | bytes 4886610 | solution.py:184
  213.3 1.4 fusion.50
  214.7 1.7 fusion.53
  216.4 1.3 convolution_add_fusion.1
  217.7 4.5 %conditional.12 = ((f32[256,128]{1,0:T(8,128)S(1)}, f32[256,128]{1,0:T(8,128)S(1)})) conditional(s32[]{:T(128)} %convert_element_type.70, (f32[256,128]{1,0:T(8,128)S(1)}, f32[256,128]{1,0:T(8,128)S(1)}) %tuple.151, (s32[]{:T(128)}, s32[]{:T(128)}, bf16[8192,128]{1,0:T(8,128)(2,1)}, bf16[256,128]{1,0:T(8,128)(2,1)S(1)}, f32[8192]{0:T(1024)S(1)}, ...), branch_computations={%region_12.12_spmd, %region_13.13_spmd} | conditional | flops 270861568 | bytes 4886610 | solution.py:184
  217.8 1.4 fusion.50
  219.2 1.7 fusion.53
  220.9 1.3 convolution_add_fusion.1
  222.2 4.5 %conditional.12 = ((f32[256,128]{1,0:T(8,128)S(1)}, f32[256,128]{1,0:T(8,128)S(1)})) conditional(s32[]{:T(128)} %convert_element_type.70, (f32[256,128]{1,0:T(8,128)S(1)}, f32[256,128]{1,0:T(8,128)S(1)}) %tuple.151, (s32[]{:T(128)}, s32[]{:T(128)}, bf16[8192,128]{1,0:T(8,128)(2,1)}, bf16[256,128]{1,0:T(8,128)(2,1)S(1)}, f32[8192]{0:T(1024)S(1)}, ...), branch_computations={%region_12.12_spmd, %region_13.13_spmd} | conditional | flops 270861568 | bytes 4886610 | solution.py:184
  222.3 1.4 fusion.50
  223.7 1.7 fusion.53
  225.4 1.3 convolution_add_fusion.1
  226.7 4.5 %conditional.12 = ((f32[256,128]{1,0:T(8,128)S(1)}, f32[256,128]{1,0:T(8,128)S(1)})) conditional(s32[]{:T(128)} %convert_element_type.70, (f32[256,128]{1,0:T(8,128)S(1)}, f32[256,128]{1,0:T(8,128)S(1)}) %tuple.151, (s32[]{:T(128)}, s32[]{:T(128)}, bf16[8192,128]{1,0:T(8,128)(2,1)}, bf16[256,128]{1,0:T(8,128)(2,1)S(1)}, f32[8192]{0:T(1024)S(1)}, ...), branch_computations={%region_12.12_spmd, %region_13.13_spmd} | conditional | flops 270861568 | bytes 4886610 | solution.py:184
  226.8 1.4 fusion.50
  228.2 1.7 fusion.53
  229.9 1.3 convolution_add_fusion.1
  231.2 4.5 %conditional.12 = ((f32[256,128]{1,0:T(8,128)S(1)}, f32[256,128]{1,0:T(8,128)S(1)})) conditional(s32[]{:T(128)} %convert_element_type.70, (f32[256,128]{1,0:T(8,128)S(1)}, f32[256,128]{1,0:T(8,128)S(1)}) %tuple.151, (s32[]{:T(128)}, s32[]{:T(128)}, bf16[8192,128]{1,0:T(8,128)(2,1)}, bf16[256,128]{1,0:T(8,128)(2,1)S(1)}, f32[8192]{0:T(1024)S(1)}, ...), branch_computations={%region_12.12_spmd, %region_13.13_spmd} | conditional | flops 270861568 | bytes 4886610 | solution.py:184
  231.3 1.4 fusion.50
  232.7 1.7 fusion.53
  234.4 1.3 convolution_add_fusion.1
  235.7 4.5 %conditional.12 = ((f32[256,128]{1,0:T(8,128)S(1)}, f32[256,128]{1,0:T(8,128)S(1)})) conditional(s32[]{:T(128)} %convert_element_type.70, (f32[256,128]{1,0:T(8,128)S(1)}, f32[256,128]{1,0:T(8,128)S(1)}) %tuple.151, (s32[]{:T(128)}, s32[]{:T(128)}, bf16[8192,128]{1,0:T(8,128)(2,1)}, bf16[256,128]{1,0:T(8,128)(2,1)S(1)}, f32[8192]{0:T(1024)S(1)}, ...), branch_computations={%region_12.12_spmd, %region_13.13_spmd} | conditional | flops 270861568 | bytes 4886610 | solution.py:184
  235.8 1.4 fusion.50
  237.2 1.7 fusion.53
  238.9 1.3 convolution_add_fusion.1
  240.2 0.6 copy-done.1
  240.8 0.0 copy-done.2
  (103 shorter events, 0.8 us)
Async XLA Ops:
  7.2 0.8 copy-start
  7.2 106.8 %copy-start.5 = (bf16[256,128]{1,0:T(8,128)(2,1)S(1)}, bf16[256,128]{1,0:T(8,128)(2,1)}, u32[]{:S(2)}) copy-start(bf16[256,128]{1,0:T(8,128)(2,1)} %param.16) | copy-start | bytes 196612
  7.2 59.2 %copy-start.4 = (bf16[256,128]{1,0:T(8,128)(2,1)S(1)}, bf16[256,128]{1,0:T(8,128)(2,1)}, u32[]{:S(2)}) copy-start(bf16[256,128]{1,0:T(8,128)(2,1)} %param.19) | copy-start | bytes 196612
  7.2 72.3 %all-gather.7.cloned.1.call-start = ((), (), s32[]{:S(2)}) async-start(), calls=%async_computation.2 | async-start | bytes 2359296 | tf_op jit(solution)/shard_map/all_gather | solution.py:19
  30.3 83.6 %all-gather.9.cloned.1.call-start = ((), (), s32[]{:S(2)}) async-start(), calls=%async_computation.3 | async-start | bytes 2359296 | tf_op jit(solution)/shard_map/all_gather | solution.py:19
  52.2 151.4 %all-gather.11.cloned.1.call-start = ((), (), s32[]{:S(2)}) async-start(), calls=%async_computation.4 | async-start | bytes 2359296 | tf_op jit(solution)/shard_map/all_gather | solution.py:19
  66.3 137.4 %all-gather.13.cloned.1.call-start = ((), (), s32[]{:S(2)}) async-start(), calls=%async_computation.5 | async-start | bytes 2359296 | tf_op jit(solution)/shard_map/all_gather | solution.py:19
  203.6 0.7 copy-start.3
  240.2 0.7 copy-start.1
  240.2 0.7 copy-start.2
Sparse Core Ops, SparseCore 0:
  30.4 42.2 all-gather.6
  74.5 39.4 all-gather.8
  115.7 39.4 all-gather.10
  156.8 39.5 all-gather.12
where the time goes:
time: 249 us; the launch traced here: 247 us
  blocking collectives  151 us (61%)
  matrix products  41.4 us (17%)
  waiting for transfers between devices  34.5 us (14%)
  between operations  14 us (6%)
  local copies, waits for them, and re-layouts  3.2 us (1%)
    all_gather x1, blocking collectives, gather_packed(): lines, at, gathered = (lax.all_gather(ravelled, axis), 0, [])  80.2 us
    all_gather x4, blocking collectives, whole_of(): filled = lax.all_gather(filled, axes[number], axis=dim, tiled=True)  53.5 us
    all_gather x4, waiting for transfers between devices, whole_of(): filled = lax.all_gather(filled, axes[number], axis=dim, tiled=True)  34.4 us
    dot_general x8, matrix products, key_compute(): jnp.einsum('qk,qd->kd', grad_scores, query_piece, preferred_element_type=...  13.6 us
    dot_general x8, matrix products, key_compute(): jnp.einsum('qd,kd->qk', query_piece, own_keys, preferred_element_type=jnp...  10.8 us
    dot_general x8, matrix products, key_compute(): jnp.einsum('qk,qd->kd', probs.astype(jnp.bfloat16), grad_piece, preferred...  10.4 us
    all_to_all x1, blocking collectives, per_device(): lax.all_to_all(keys, 'head', split_axis=1, concat_axis=0, tiled=True)  8.88 us
    all_to_all x1, blocking collectives, per_device(): lax.all_to_all(values, 'head', split_axis=1, concat_axis=0, tiled=True)  8 us
  transfers between devices with their start and end apart: 4, of which 1 were waited for; matrix products, arithmetic and copies ran while one was open for 4% of the time, Pallas kernels for 0%

commit v1 on v0

v1 whole, which is shorter than its diff:
```python
import functools
import math

import jax
import jax.numpy as jnp
from jax import lax
from jax.experimental import pallas as pl
from jax.experimental.pallas import tpu as pltpu
from jax.sharding import Mesh
from jax.sharding import PartitionSpec as P

SEQ = ("z", "x")
SEQ_HEAD = ("z", "x", "head")
LOW = -1e30
F32 = jnp.float32
BF16 = jnp.bfloat16
NT = (((1,), (1,)), ((), ()))
TN = (((0,), (0,)), ((), ()))
NN = (((1,), (0,)), ((), ()))


def dot(a, b, dims):
    return lax.dot_general(a, b, dims, preferred_element_type=F32)


def allowed_pairs(rows, key_block, query_block):
    key_pos = lax.broadcasted_iota(jnp.int32, (rows, rows), 0) + key_block * rows
    query_pos = lax.broadcasted_iota(jnp.int32, (rows, rows), 1) + query_block * rows
    return key_pos <= query_pos


def forward_kernel(rate, nx, where_ref, *refs):
    q_refs, (kv_ref, o_ref, stat_ref, m_ref, l_ref) = refs[:nx], refs[nx:]
    z, x = where_ref[0], where_ref[1]
    rows, width = kv_ref.shape[1], kv_ref.shape[2] // 2
    m_ref[...] = jnp.full_like(m_ref, LOW)
    l_ref[...] = jnp.zeros_like(l_ref)
    o_ref[...] = jnp.zeros_like(o_ref)

    def unit(j, masked):
        k, v = kv_ref[j, :, :width], kv_ref[j, :, width:]
        for r in range(nx):
            cols = slice(r * rows, (r + 1) * rows)
            s = dot(k, q_refs[r][:, :width], NT)
            if masked:
                ok = allowed_pairs(rows, x, lax.rem(x - r + nx, nx))
                s = jnp.where(ok, s, LOW)
            m_old = m_ref[:, cols]
            m_new = jnp.maximum(m_old, jnp.max(s, axis=0, keepdims=True))
            p = jnp.exp2((s - m_new) * rate)
            if masked:
                p = jnp.where(ok, p, 0.0)
            alpha = jnp.exp2((m_old - m_new) * rate)
            m_ref[:, cols] = m_new
            l_ref[:, cols] = l_ref[:, cols] * alpha + jnp.sum(p, axis=0, keepdims=True)
            o_ref[:, cols] = o_ref[:, cols] * alpha + dot(v, p.astype(BF16), TN)

    @pl.loop(0, z)
    def _(j):
        unit(j, False)

    unit(z, True)
    for r in range(nx):
        cols = slice(r * rows, (r + 1) * rows)
        grads = jnp.transpose(q_refs[r][:, width:].astype(F32))
        at = lax.rem(x - r + nx, nx)
        stat_ref[at, 0:1, :] = m_ref[:, cols] * rate
        stat_ref[at, 1:2, :] = l_ref[:, cols]
        stat_ref[at, 2:3, :] = jnp.sum(grads * o_ref[:, cols], axis=0, keepdims=True)


def backward_kernel(rate, scaling, nx, where_ref, *refs):
    q_refs, (kv_ref, o_ref, stat_ref), refs = refs[:nx], refs[nx : nx + 3], refs[nx + 3 :]
    out_refs, (dkv_ref, dq_ref, norm_ref, delta_ref) = refs[:nx], refs[nx:]
    z, x = where_ref[0], where_ref[1]
    rows, width = kv_ref.shape[1], kv_ref.shape[2] // 2
    dq_ref[...] = jnp.zeros_like(dq_ref)
    for r in range(nx):
        cols = slice(r * rows, (r + 1) * rows)
        at = lax.rem(x - r + nx, nx)
        maxima = [stat_ref[i, at, 0:1, :] for i in range(nx)]
        top = functools.reduce(jnp.maximum, maxima)
        shares = [jnp.exp2(m - top) for m in maxima]
        total = sum(stat_ref[i, at, 1:2, :] * shares[i] for i in range(nx))
        delta = sum(stat_ref[i, at, 2:3, :] * shares[i] for i in range(nx))
        norm = top + jnp.log2(total)
        norm_ref[:, cols] = norm
        delta_ref[:, cols] = delta / total
        own = stat_ref[x, at, 0:1, :]
        mine = o_ref[:, cols] * (jnp.exp2(own - top) / total)
        out_refs[r][:, width:] = jnp.transpose(mine).astype(BF16)

    def unit(j, masked):
        k, v = kv_ref[j, :, :width], kv_ref[j, :, width:]
        dk = jnp.zeros((rows, width), F32)
        dv = jnp.zeros((rows, width), F32)
        for r in range(nx):
            cols = slice(r * rows, (r + 1) * rows)
            q, g = q_refs[r][:, :width], q_refs[r][:, width:]
            s = dot(k, q, NT)
            p = jnp.exp2(s * rate - norm_ref[:, cols])
            if masked:
                p = jnp.where(allowed_pairs(rows, x, lax.rem(x - r + nx, nx)), p, 0.0)
            ds = (p * (dot(v, g, NT) - delta_ref[:, cols])).astype(BF16)
            dv = dv + dot(p.astype(BF16), g, NN)
            dk = dk + dot(ds, q, NN)
            dq_ref[:, cols] += dot(k, ds, TN)
        dkv_ref[j, :, :width] = (dk * scaling).astype(BF16)
        dkv_ref[j, :, width:] = dv.astype(BF16)

    @pl.loop(0, z)
    def _(j):
        unit(j, False)

    unit(z, True)

    @pl.loop(z + 1, kv_ref.shape[0])
    def _(j):
        dkv_ref[j] = jnp.zeros(kv_ref.shape[1:], BF16)

    for r in range(nx):
        cols = slice(r * rows, (r + 1) * rows)
        out_refs[r][:, :width] = jnp.transpose(dq_ref[:, cols] * scaling).astype(BF16)


def shifted(value, axis, count, step):
    return lax.ppermute(value, axis, [(i, (i + step) % count) for i in range(count)])


def per_device(nz, nx, nh, queries, keys, values, out_grad):
    rows, width = queries.shape
    scaling = 1.0 / math.sqrt(width)
    rate = scaling * math.log2(math.e)
    smem = pl.BlockSpec(memory_space=pltpu.SMEM)
    vmem = pl.BlockSpec(memory_space=pltpu.VMEM)
    own = jnp.concatenate([queries, out_grad], axis=1)
    blocks = [own] + [shifted(own, "x", nx, r) for r in range(1, nx)]
    mixed = jnp.concatenate(
        [keys.reshape(-1, nh, width), values.reshape(-1, nh, width)], axis=2
    ).transpose(1, 0, 2)
    local = lax.all_to_all(mixed, "head", 0, 0, tiled=True).reshape(rows, 2 * width)
    kv = lax.all_to_all(jnp.broadcast_to(local, (nz, *local.shape)), "z", 0, 0, tiled=True)
    where = jnp.stack([lax.axis_index("z"), lax.axis_index("x")]).astype(jnp.int32)
    pairs = nz * rows * nx * rows * width
    partial, stats = pl.pallas_call(
        functools.partial(forward_kernel, rate, nx),
        out_shape=(
            jax.ShapeDtypeStruct((width, nx * rows), F32),
            jax.ShapeDtypeStruct((nx, 8, rows), F32),
        ),
        in_specs=[smem] + [vmem] * (nx + 1),
        out_specs=(vmem, vmem),
        scratch_shapes=[pltpu.VMEM((1, nx * rows), F32), pltpu.VMEM((1, nx * rows), F32)],
        cost_estimate=pl.CostEstimate(flops=4 * pairs, bytes_accessed=2 << 20, transcendentals=0),
        name="forward",
    )(where, *blocks, kv)
    stats = lax.all_to_all(jnp.broadcast_to(stats, (nx, *stats.shape)), "x", 0, 0, tiled=True)
    *parts, dkv = pl.pallas_call(
        functools.partial(backward_kernel, rate, scaling, nx),
        out_shape=tuple(jax.ShapeDtypeStruct((rows, 2 * width), BF16) for _ in range(nx))
        + (jax.ShapeDtypeStruct(kv.shape, BF16),),
        in_specs=[smem] + [vmem] * (nx + 3),
        out_specs=(vmem,) * (nx + 1),
        scratch_shapes=[
            pltpu.VMEM((width, nx * rows), F32),
            pltpu.VMEM((1, nx * rows), F32),
            pltpu.VMEM((1, nx * rows), F32),
        ],
        cost_estimate=pl.CostEstimate(flops=10 * pairs, bytes_accessed=2 << 20, transcendentals=0),
        name="backward",
    )(where, *blocks, kv, partial, stats)
    arrived = [shifted(parts[-r % nx], "x", nx, r) for r in range(1, nx)]
    dkv = lax.all_to_all(dkv, "z", 0, 0, tiled=True)
    dkv = jnp.sum(dkv.astype(F32), axis=0)
    total = functools.reduce(jnp.add, [a.astype(F32) for a in [parts[0], *arrived]])
    return total[:, width:].astype(BF16), total[:, :width], dkv[:, :width], dkv[:, width:]


def solution(mesh):
    nh = mesh.shape["head"]
    split = Mesh(mesh.devices.reshape(8, -1, nh), SEQ_HEAD)
    return jax.shard_map(
        functools.partial(per_device, 8, split.shape["x"], nh),
        mesh=split,
        in_specs=(P(SEQ, "head"), P(SEQ_HEAD, None), P(SEQ_HEAD, None), P(SEQ, "head")),
        out_specs=(P(SEQ, "head"),) * 4,
        check_vma=False,
    )
```

time: 249 us -> 115 us (0.46)
  blocking collectives: 151 us -> 19.5 us
  matrix products: 41.4 us -> 0 us
  starting transfers between devices: 0.16 us -> 33.3 us
  between operations: 14 us -> 0.75 us
  waiting for transfers between devices: 34.5 us -> 45.2 us
  Pallas kernels: 0 us -> 7.89 us
  local copies, waits for them, and re-layouts: 3.2 us -> 6.62 us
    all_gather x5 -> x0, blocking collectives: 134 us -> none  [the longest x1 80.2 us: gather_packed(): lines, at, gathered = (lax.all_gather(ravelled, axis), 0, [])]
    dot_general x28 -> x0, matrix products: 41.4 us -> none  [the longest x8 13.6 us: key_compute(): jnp.einsum('qk,qd->kd', grad_scores, query_piece, preferred_element_type=...]
    all_gather x4 -> x0, waiting for transfers between devices: 34.4 us -> none  [whole_of(): filled = lax.all_gather(filled, axes[number], axis=dim, tiled=True)]
    all_to_all x0 -> x2, waiting for transfers between devices: none -> 33.7 us  [the longest x1 16.9 us: per_device(): dkv = lax.all_to_all(dkv, 'z', 0, 0, tiled=True)]
    all_to_all x0 -> x2, starting transfers between devices: none -> 25.2 us  [the longest x1 16.6 us: per_device(): dkv = lax.all_to_all(dkv, 'z', 0, 0, tiled=True)]
    ppermute x0 -> x6, waiting for transfers between devices: none -> 11.5 us  [shifted(): lax.ppermute(value, axis, [(i, (i + step) % count) for i in range(count)])]
    ppermute x0 -> x6, starting transfers between devices: none -> 8.11 us  [shifted(): lax.ppermute(value, axis, [(i, (i + step) % count) for i in range(count)])]
    pallas_call x0 -> x2, Pallas kernels: none -> 7.89 us  [the longest x1 4.22 us: per_device(): pl.pallas_call(functools.partial(backward_kernel, rate, scaling, nx), out...]
  transfers between devices with their start and end apart: 4 -> 8, of which waited for: 1 -> 7; matrix products, arithmetic and copies ran while one was open for 4% -> 2% of each run, Pallas kernels for 0% -> 0%
where the time goes in v1:
time: 115 us; the launch traced here: 114 us
  waiting for transfers between devices  45.2 us (39%)
  starting transfers between devices  33.3 us (29%)
  blocking collectives  19.5 us (17%)
  Pallas kernels  7.89 us (7%)
  local copies, waits for them, and re-layouts  6.62 us (6%)
    all_to_all x1, waiting for transfers between devices, per_device(): dkv = lax.all_to_all(dkv, 'z', 0, 0, tiled=True)  16.9 us
    all_to_all x1, waiting for transfers between devices, per_device(): lax.all_to_all(jnp.broadcast_to(local, (nz, *local.shape)), 'z', 0, 0, ti...  16.8 us
    all_to_all x1, starting transfers between devices, per_device(): dkv = lax.all_to_all(dkv, 'z', 0, 0, tiled=True)  16.6 us
    ppermute x6, waiting for transfers between devices, shifted(): lax.ppermute(value, axis, [(i, (i + step) % count) for i in range(count)])  11.5 us
    all_to_all x1, blocking collectives, per_device(): lax.all_to_all(jnp.broadcast_to(stats, (nx, *stats.shape)), 'x', 0, 0, ti...  10.2 us
    all_to_all x1, blocking collectives, per_device(): lax.all_to_all(mixed, 'head', 0, 0, tiled=True).reshape(rows, 2 * width)  9.36 us
    all_to_all x1, starting transfers between devices, per_device(): lax.all_to_all(jnp.broadcast_to(local, (nz, *local.shape)), 'z', 0, 0, ti...  8.6 us
    ppermute x6, starting transfers between devices, shifted(): lax.ppermute(value, axis, [(i, (i + step) % count) for i in range(count)])  8.11 us
  transfers between devices with their start and end apart: 8, of which 7 were waited for; matrix products, arithmetic and copies ran while one was open for 2% of the time, Pallas kernels for 0%

profile of v1, /device:TPU:8, one launch (start us, length us, event | category | flops | bytes accessed | tf_op | source)
XLA Modules:
  0.0 114.1 jit_solution(8954232663525920194)
XLA Ops:
  0.6 0.9 copy.10
  1.5 0.9 copy.11
  2.4 9.4 %all_to_all.20 = bf16[8,32,256]{2,1,0:T(8,128)(2,1)S(1)} all-to-all(bf16[8,32,256]{2,1,0:T(8,128)(2,1)S(1)} %copy.9), channel_id=1, replica_groups=mesh['z'=8,'x'=4,'head'=8] {'head'}, dimensions={0} | all-to-all | bytes 262144 | tf_op jit(solution)/shard_map/all_to_all | solution.py:141
  11.8 1.1 broadcast_in_dim.6
  12.8 0.0 copy-start.2
  12.8 0.0 copy-start.3
  12.8 8.6 %all-to-all-start.1 = ((bf16[8,256,256]{2,1,0:T(8,128)(2,1)}), bf16[8,256,256]{2,1,0:T(8,128)(2,1)S(1)}, u32[]{:S(2)}, u32[]{:S(2)}) async-start(bf16[8,256,256]{2,1,0:T(8,128)(2,1)} %broadcast_in_dim.6), calls=%async_computation.1 | async-start | bytes 2097152 | tf_op jit(solution)/shard_map/all_to_all | solution.py:142
  21.4 0.0 copy-done.2
  21.4 0.0 copy-done.3
  21.5 0.0 copy-start.4
  21.5 2.8 %collective-permute-start.2 = (bf16[256,256]{1,0:T(8,128)(2,1)S(1)}, bf16[256,256]{1,0:T(8,128)(2,1)S(1)}, u32[]{:S(2)}, u32[]{:S(2)}) collective-permute-start(bf16[256,256]{1,0:T(8,128)(2,1)S(1)} %constant_dynamic-update-slice_fusion.refs_0_), channel_id=1, source_target_pairs={{0,24},{8,0},{16,8},{24,16},{1,25},{9,1},{17,9},{25,17},{2,26},{10... | collective-permute-start | bytes 393224 | tf_op jit(solution)/shard_map/ppermute | solution.py:127
  24.3 0.8 collective-permute-start.1
  25.1 0.9 collective-permute-start
  26.0 0.6 pad_add_fusion.where_ref
  26.6 2.9 %collective-permute-done.2.refs_3_ = bf16[256,256]{1,0:T(8,128)(2,1)S(1)} collective-permute-done((bf16[256,256]{1,0:T(8,128)(2,1)S(1)}, bf16[256,256]{1,0:T(8,128)(2,1)S(1)}, u32[]{:S(2)}, u32[]{:S(2)}) %collective-permute-start.2) | collective-permute-done | bytes 131104 | tf_op jit(solution)/shard_map/ppermute | solution.py:127
  29.5 0.0 copy-start.5
  29.5 2.3 %collective-permute-done.1.refs_2_ = bf16[256,256]{1,0:T(8,128)(2,1)S(1)} collective-permute-done((bf16[256,256]{1,0:T(8,128)(2,1)S(1)}, bf16[256,256]{1,0:T(8,128)(2,1)S(1)}, u32[]{:S(2)}, u32[]{:S(2)}) %collective-permute-start.1) | collective-permute-done | bytes 131104 | tf_op jit(solution)/shard_map/ppermute | solution.py:127
  31.7 0.0 copy-start.6
  31.7 1.4 %collective-permute-done.refs_1_ = bf16[256,256]{1,0:T(8,128)(2,1)S(1)} collective-permute-done((bf16[256,256]{1,0:T(8,128)(2,1)S(1)}, bf16[256,256]{1,0:T(8,128)(2,1)S(1)}, u32[]{:S(2)}, u32[]{:S(2)}) %collective-permute-start) | collective-permute-done | bytes 131104 | tf_op jit(solution)/shard_map/ppermute | solution.py:127
  33.1 0.0 copy-start.7
  33.1 16.8 %all-to-all-done.1.refs_4_ = bf16[8,256,256]{2,1,0:T(8,128)(2,1)S(1)} async-done(((bf16[8,256,256]{2,1,0:T(8,128)(2,1)}), bf16[8,256,256]{2,1,0:T(8,128)(2,1)S(1)}, u32[]{:S(2)}, u32[]{:S(2)}) %all-to-all-start.1) | async-done | bytes 1048608 | tf_op jit(solution)/shard_map/all_to_all | solution.py:142
  50.0 0.0 copy-done.4
  50.0 0.0 copy-done.5
  50.0 0.0 copy-done.6
  50.0 0.0 copy-done.7
  50.0 0.0 copy-start
  50.0 1.0 copy-done
  51.0 3.7 %forward.1 = (f32[128,1024]{1,0:T(8,128)}, f32[4,8,256]{2,1,0:T(8,128)}) custom-call(s32[2]{0:T(128)} %pad_add_fusion.where_ref, bf16[256,256]{1,0:T(8,128)(2,1)} %copy-done.4, bf16[256,256]{1,0:T(8,128)(2,1)} %copy-done.7, bf16[256,256]{1,0:T(8,128)(2,1)} %copy-done.6, bf16[256,256]{1,0:T(8,128)(2,1)} %copy-done.5, bf16[8,256,256]{2,1,0:T(8,128)(2,1)} %copy-done), custom_call_target="tpu_custom_call" | custom-call | flops 1073741824 | bytes 2097152 | tf_op jit(solution)/shard_map/forward/pallas_call | solution.py:145
  54.6 0.8 broadcast_in_dim.7
  55.4 10.2 %all_to_all.21.refs_6_ = f32[4,4,8,256]{3,2,1,0:T(8,128)} all-to-all(f32[4,4,8,256]{3,2,1,0:T(8,128)S(1)} %broadcast_in_dim.7), channel_id=1, replica_groups=mesh['z'=8,'x'=4,'head'=8] {'x'}, dimensions={0} | all-to-all | bytes 262144 | tf_op jit(solution)/shard_map/all_to_all | solution.py:157
  65.6 4.2 %backward.1 = (bf16[256,256]{1,0:T(8,128)(2,1)}, bf16[256,256]{1,0:T(8,128)(2,1)}, bf16[256,256]{1,0:T(8,128)(2,1)}, bf16[256,256]{1,0:T(8,128)(2,1)}, bf16[8,256,256]{2,1,0:T(8,128)(2,1)}) custom-call(s32[2]{0:T(128)} %pad_add_fusion.where_ref, bf16[256,256]{1,0:T(8,128)(2,1)} %copy-done.4, bf16[256,256]{1,0:T(8,128)(2,1)} %copy-done.7, ...), custom_call_target="tpu_custom_call" | custom-call | flops 2684354560 | bytes 2097152 | tf_op jit(solution)/shard_map/backward/pallas_call | solution.py:158
  69.8 0.0 copy-start.10
  69.8 0.0 copy-start.9
  69.8 0.0 copy-start.8
  69.8 0.0 copy-start.1
  69.8 16.6 %all-to-all-start.3 = ((bf16[8,256,256]{2,1,0:T(8,128)(2,1)}), bf16[8,256,256]{2,1,0:T(8,128)(2,1)S(1)}, u32[]{:S(2)}, u32[]{:S(2)}) async-start(bf16[8,256,256]{2,1,0:T(8,128)(2,1)} %get-tuple-element.17), calls=%async_computation.3 | async-start | bytes 2097152 | tf_op jit(solution)/shard_map/all_to_all | solution.py:173
  86.4 0.0 copy-done.10
  86.4 0.7 collective-permute-start.3
  87.1 0.0 copy-done.9
  87.1 2.0 %collective-permute-start.4 = (bf16[256,256]{1,0:T(8,128)(2,1)S(1)}, bf16[256,256]{1,0:T(8,128)(2,1)S(1)}, u32[]{:S(2)}, u32[]{:S(2)}) collective-permute-start(bf16[256,256]{1,0:T(8,128)(2,1)S(1)} %copy-done.9), channel_id=1, source_target_pairs={{0,16},{8,24},{16,0},{24,8},{1,17},{9,25},{17,1},{25,9},{2,18},{10... | collective-permute-start | bytes 393224 | tf_op jit(solution)/shard_map/ppermute | solution.py:127
  89.1 0.0 copy-done.8
  89.1 0.9 collective-permute-start.5
  90.0 4.1 %collective-permute-done.3 = bf16[256,256]{1,0:T(8,128)(2,1)S(1)} collective-permute-done((bf16[256,256]{1,0:T(8,128)(2,1)S(1)}, bf16[256,256]{1,0:T(8,128)(2,1)S(1)}, u32[]{:S(2)}, u32[]{:S(2)}) %collective-permute-start.3) | collective-permute-done | bytes 131104 | tf_op jit(solution)/shard_map/ppermute | solution.py:127
  94.1 0.0 collective-permute-done.4
  94.1 0.9 collective-permute-done.5
  95.0 0.0 copy-done.1
  95.0 0.1 convert_add_fusion
  95.0 0.6 slice.22
  95.7 0.7 slice.18
  96.3 16.9 %all-to-all-done.3 = bf16[8,256,256]{2,1,0:T(8,128)(2,1)S(1)} async-done(((bf16[8,256,256]{2,1,0:T(8,128)(2,1)}), bf16[8,256,256]{2,1,0:T(8,128)(2,1)S(1)}, u32[]{:S(2)}, u32[]{:S(2)}) %all-to-all-start.3) | async-done | bytes 1048608 | tf_op jit(solution)/shard_map/all_to_all | solution.py:173
  113.2 0.1 convert_reduce_fusion
  113.4 0.7 fusion
  (4 shorter events, 0.1 us)
Async XLA Ops:
  12.8 8.6 %copy-start.2 = (bf16[256,128]{1,0:T(8,128)(2,1)S(1)}, bf16[256,128]{1,0:T(8,128)(2,1)}, u32[]{:S(2)}) copy-start(bf16[256,128]{1,0:T(8,128)(2,1)} %param.4) | copy-start | bytes 196612
  12.8 8.6 %copy-start.3 = (bf16[256,128]{1,0:T(8,128)(2,1)S(1)}, bf16[256,128]{1,0:T(8,128)(2,1)}, u32[]{:S(2)}) copy-start(bf16[256,128]{1,0:T(8,128)(2,1)} %param.7) | copy-start | bytes 196612
  12.8 37.1 %all-to-all-start.1 = ((bf16[8,256,256]{2,1,0:T(8,128)(2,1)}), bf16[8,256,256]{2,1,0:T(8,128)(2,1)S(1)}, u32[]{:S(2)}, u32[]{:S(2)}) async-start(bf16[8,256,256]{2,1,0:T(8,128)(2,1)} %broadcast_in_dim.6), calls=%async_computation.1 | async-start | bytes 2097152 | tf_op jit(solution)/shard_map/all_to_all | solution.py:142
  21.5 28.5 %copy-start.4 = (bf16[256,256]{1,0:T(8,128)(2,1)}, bf16[256,256]{1,0:T(8,128)(2,1)S(1)}, u32[]{:S(2)}) copy-start(bf16[256,256]{1,0:T(8,128)(2,1)S(1)} %constant_dynamic-update-slice_fusion.refs_0_) | copy-start | bytes 393220
  21.5 8.0 %collective-permute-start.2 = (bf16[256,256]{1,0:T(8,128)(2,1)S(1)}, bf16[256,256]{1,0:T(8,128)(2,1)S(1)}, u32[]{:S(2)}, u32[]{:S(2)}) collective-permute-start(bf16[256,256]{1,0:T(8,128)(2,1)S(1)} %constant_dynamic-update-slice_fusion.refs_0_), channel_id=1, source_target_pairs={{0,24},{8,0},{16,8},{24,16},{1,25},{9,1},{17,9},{25,17},{2,26},{10... | collective-permute-start | bytes 393224 | tf_op jit(solution)/shard_map/ppermute | solution.py:127
  24.3 7.4 %collective-permute-start.1 = (bf16[256,256]{1,0:T(8,128)(2,1)S(1)}, bf16[256,256]{1,0:T(8,128)(2,1)S(1)}, u32[]{:S(2)}, u32[]{:S(2)}) collective-permute-start(bf16[256,256]{1,0:T(8,128)(2,1)S(1)} %constant_dynamic-update-slice_fusion.refs_0_), channel_id=1, source_target_pairs={{0,16},{8,24},{16,0},{24,8},{1,17},{9,25},{17,1},{25,9},{2,18},{10... | collective-permute-start | bytes 393224 | tf_op jit(solution)/shard_map/ppermute | solution.py:127
  25.1 8.0 %collective-permute-start = (bf16[256,256]{1,0:T(8,128)(2,1)S(1)}, bf16[256,256]{1,0:T(8,128)(2,1)S(1)}, u32[]{:S(2)}, u32[]{:S(2)}) collective-permute-start(bf16[256,256]{1,0:T(8,128)(2,1)S(1)} %constant_dynamic-update-slice_fusion.refs_0_), channel_id=1, source_target_pairs={{0,8},{8,16},{16,24},{24,0},{1,9},{9,17},{17,25},{25,1},{2,10},{10... | collective-permute-start | bytes 393224 | tf_op jit(solution)/shard_map/ppermute | solution.py:127
  29.5 20.5 %copy-start.5 = (bf16[256,256]{1,0:T(8,128)(2,1)}, bf16[256,256]{1,0:T(8,128)(2,1)S(1)}, u32[]{:S(2)}) copy-start(bf16[256,256]{1,0:T(8,128)(2,1)S(1)} %collective-permute-done.2.refs_3_) | copy-start | bytes 393220
  31.7 18.2 %copy-start.6 = (bf16[256,256]{1,0:T(8,128)(2,1)}, bf16[256,256]{1,0:T(8,128)(2,1)S(1)}, u32[]{:S(2)}) copy-start(bf16[256,256]{1,0:T(8,128)(2,1)S(1)} %collective-permute-done.1.refs_2_) | copy-start | bytes 393220
  33.1 16.8 %copy-start.7 = (bf16[256,256]{1,0:T(8,128)(2,1)}, bf16[256,256]{1,0:T(8,128)(2,1)S(1)}, u32[]{:S(2)}) copy-start(bf16[256,256]{1,0:T(8,128)(2,1)S(1)} %collective-permute-done.refs_1_) | copy-start | bytes 393220
  50.0 1.0 copy-start
  69.8 16.6 %copy-start.10 = (bf16[256,256]{1,0:T(8,128)(2,1)S(1)}, bf16[256,256]{1,0:T(8,128)(2,1)}, u32[]{:S(2)}) copy-start(bf16[256,256]{1,0:T(8,128)(2,1)} %get-tuple-element.14) | copy-start | bytes 393220
  69.8 17.3 %copy-start.9 = (bf16[256,256]{1,0:T(8,128)(2,1)S(1)}, bf16[256,256]{1,0:T(8,128)(2,1)}, u32[]{:S(2)}) copy-start(bf16[256,256]{1,0:T(8,128)(2,1)} %get-tuple-element.15) | copy-start | bytes 393220
  69.8 19.3 %copy-start.8 = (bf16[256,256]{1,0:T(8,128)(2,1)S(1)}, bf16[256,256]{1,0:T(8,128)(2,1)}, u32[]{:S(2)}) copy-start(bf16[256,256]{1,0:T(8,128)(2,1)} %get-tuple-element.16) | copy-start | bytes 393220
  69.8 25.1 %copy-start.1 = (bf16[256,256]{1,0:T(8,128)(2,1)S(1)}, bf16[256,256]{1,0:T(8,128)(2,1)}, u32[]{:S(2)}) copy-start(bf16[256,256]{1,0:T(8,128)(2,1)} %get-tuple-element.13) | copy-start | bytes 393220
  69.8 43.4 %all-to-all-start.3 = ((bf16[8,256,256]{2,1,0:T(8,128)(2,1)}), bf16[8,256,256]{2,1,0:T(8,128)(2,1)S(1)}, u32[]{:S(2)}, u32[]{:S(2)}) async-start(bf16[8,256,256]{2,1,0:T(8,128)(2,1)} %get-tuple-element.17), calls=%async_computation.3 | async-start | bytes 2097152 | tf_op jit(solution)/shard_map/all_to_all | solution.py:173
  86.4 7.7 %collective-permute-start.3 = (bf16[256,256]{1,0:T(8,128)(2,1)S(1)}, bf16[256,256]{1,0:T(8,128)(2,1)S(1)}, u32[]{:S(2)}, u32[]{:S(2)}) collective-permute-start(bf16[256,256]{1,0:T(8,128)(2,1)S(1)} %copy-done.10), channel_id=1, source_target_pairs={{0,8},{8,16},{16,24},{24,0},{1,9},{9,17},{17,25},{25,1},{2,10},{10... | collective-permute-start | bytes 393224 | tf_op jit(solution)/shard_map/ppermute | solution.py:127
  87.1 7.0 %collective-permute-start.4 = (bf16[256,256]{1,0:T(8,128)(2,1)S(1)}, bf16[256,256]{1,0:T(8,128)(2,1)S(1)}, u32[]{:S(2)}, u32[]{:S(2)}) collective-permute-start(bf16[256,256]{1,0:T(8,128)(2,1)S(1)} %copy-done.9), channel_id=1, source_target_pairs={{0,16},{8,24},{16,0},{24,8},{1,17},{9,25},{17,1},{25,9},{2,18},{10... | collective-permute-start | bytes 393224 | tf_op jit(solution)/shard_map/ppermute | solution.py:127
  89.1 5.8 %collective-permute-start.5 = (bf16[256,256]{1,0:T(8,128)(2,1)S(1)}, bf16[256,256]{1,0:T(8,128)(2,1)S(1)}, u32[]{:S(2)}, u32[]{:S(2)}) collective-permute-start(bf16[256,256]{1,0:T(8,128)(2,1)S(1)} %copy-done.8), channel_id=1, source_target_pairs={{0,24},{8,0},{16,8},{24,16},{1,25},{9,1},{17,9},{25,17},{2,26},{10... | collective-permute-start | bytes 393224 | tf_op jit(solution)/shard_map/ppermute | solution.py:127

commit v2 on v1

v2 whole, which is shorter than its diff:
```python
import functools
import math

import jax
import jax.numpy as jnp
from jax import lax
from jax.experimental import pallas as pl
from jax.experimental.pallas import tpu as pltpu
from jax.sharding import Mesh
from jax.sharding import PartitionSpec as P

Z = ("zj", "zp")
SEQ = (*Z, "x")
VMEM = 24 << 20
LOW = -1e30
F32 = jnp.float32
BF16 = jnp.bfloat16
NT = (((1,), (1,)), ((), ()))
TN = (((0,), (0,)), ((), ()))
NN = (((1,), (0,)), ((), ()))


def dot(a, b, dims):
    return lax.dot_general(a, b, dims, preferred_element_type=F32)


def allowed_pairs(rows, key_block, query_block):
    key_pos = lax.broadcasted_iota(jnp.int32, (rows, rows), 0) + key_block * rows
    query_pos = lax.broadcasted_iota(jnp.int32, (rows, rows), 1) + query_block * rows
    return key_pos <= query_pos


def spans(where_ref):
    zj, zp = where_ref[0], where_ref[1]
    return zj, 4 - zp - zj


def forward_kernel(rate, nx, where_ref, *refs):
    q_refs, (kv_ref, o_ref, stat_ref, m_ref, l_ref) = refs[: 2 * nx], refs[2 * nx :]
    x, high = where_ref[2], where_ref[3]
    own, mirror = spans(where_ref)
    rows, width = kv_ref.shape[1], kv_ref.shape[2] // 2
    m_ref[...] = jnp.full_like(m_ref, LOW)
    l_ref[...] = jnp.zeros_like(l_ref)
    o_ref[...] = jnp.zeros_like(o_ref)

    def unit(side, j, masked):
        k, v = kv_ref[j, :, :width], kv_ref[j, :, width:]
        for r in range(nx):
            at = side * nx + r
            cols = slice(at * rows, (at + 1) * rows)
            s = dot(k, q_refs[at][:, :width], NT)
            if masked:
                ok = allowed_pairs(rows, x, lax.rem(x - r + nx, nx))
                s = jnp.where(ok, s, LOW)
            m_old = m_ref[:, cols]
            m_new = jnp.maximum(m_old, jnp.max(s, axis=0, keepdims=True))
            p = jnp.exp2((s - m_new) * rate)
            if masked:
                p = jnp.where(ok, p, 0.0)
            alpha = jnp.exp2((m_old - m_new) * rate)
            m_ref[:, cols] = m_new
            l_ref[:, cols] = l_ref[:, cols] * alpha + jnp.sum(p, axis=0, keepdims=True)
            o_ref[:, cols] = o_ref[:, cols] * alpha + dot(v, p.astype(BF16), TN)

    @pl.loop(0, own)
    def _(j):
        unit(0, j, False)

    unit(0, own, True)

    @pl.loop(0, mirror)
    def _(j):
        unit(1, j, False)

    for at in range(2 * nx):
        side, r = divmod(at, nx)
        cols = slice(at * rows, (at + 1) * rows)
        grads = jnp.transpose(q_refs[at][:, width:].astype(F32))
        to = lax.rem(x - r + nx, nx)
        end = side ^ high
        stat_ref[end, to, 0:1, :] = m_ref[:, cols] * rate
        stat_ref[end, to, 1:2, :] = l_ref[:, cols]
        stat_ref[end, to, 2:3, :] = jnp.sum(grads * o_ref[:, cols], axis=0, keepdims=True)


def backward_kernel(rate, scaling, nx, where_ref, *refs):
    n = 2 * nx
    q_refs, (kv_ref, o_ref, mine_ref, stat_ref), refs = refs[:n], refs[n : n + 4], refs[n + 4 :]
    out_refs, (dkv_ref, dq_ref, norm_ref, delta_ref, acc_ref) = refs[:nx], refs[nx:]
    x, high = where_ref[2], where_ref[3]
    own, mirror = spans(where_ref)
    rows, width = kv_ref.shape[1], kv_ref.shape[2] // 2
    dq_ref[...] = jnp.zeros_like(dq_ref)
    acc_ref[...] = jnp.zeros_like(acc_ref)
    for at in range(n):
        side, r = divmod(at, nx)
        cols = slice(at * rows, (at + 1) * rows)
        here = lax.rem(x - r + nx, nx)
        end = side ^ high
        maxima = [stat_ref[i, end, here, 0:1, :] for i in range(n)]
        top = functools.reduce(jnp.maximum, maxima)
        shares = [jnp.exp2(m - top) for m in maxima]
        total = sum(stat_ref[i, end, here, 1:2, :] * w for i, w in enumerate(shares))
        delta = sum(stat_ref[i, end, here, 2:3, :] * w for i, w in enumerate(shares))
        norm_ref[:, cols] = top + jnp.log2(total)
        delta_ref[:, cols] = delta / total
        share = jnp.exp2(mine_ref[end, here, 0:1, :] - top) / total
        out_refs[r][side * rows : (side + 1) * rows, width:] = jnp.transpose(
            o_ref[:, cols] * share
        ).astype(BF16)

    def unit(side, j, masked):
        k, v = kv_ref[j, :, :width], kv_ref[j, :, width:]
        dk = jnp.zeros((rows, width), F32)
        dv = jnp.zeros((rows, width), F32)
        for r in range(nx):
            at = side * nx + r
            cols = slice(at * rows, (at + 1) * rows)
            q, g = q_refs[at][:, :width], q_refs[at][:, width:]
            p = jnp.exp2(dot(k, q, NT) * rate - norm_ref[:, cols])
            if masked:
                p = jnp.where(allowed_pairs(rows, x, lax.rem(x - r + nx, nx)), p, 0.0)
            ds = (p * (dot(v, g, NT) - delta_ref[:, cols])).astype(BF16)
            dv = dv + dot(p.astype(BF16), g, NN)
            dk = dk + dot(ds, q, NN)
            dq_ref[:, cols] += dot(k, ds, TN)
        acc_ref[j, :, :width] += dk
        acc_ref[j, :, width:] += dv

    @pl.loop(0, own)
    def _(j):
        unit(0, j, False)

    unit(0, own, True)

    @pl.loop(0, mirror)
    def _(j):
        unit(1, j, False)

    dkv_ref[:, :, :width] = (acc_ref[:, :, :width] * scaling).astype(BF16)
    dkv_ref[:, :, width:] = acc_ref[:, :, width:].astype(BF16)
    for at in range(n):
        side, r = divmod(at, nx)
        cols = slice(at * rows, (at + 1) * rows)
        out_refs[r][side * rows : (side + 1) * rows, :width] = jnp.transpose(
            dq_ref[:, cols] * scaling
        ).astype(BF16)


def shifted(value, axis, count, step):
    return lax.ppermute(value, axis, [(i, (i + step) % count) for i in range(count)])


def mirrored(value, count):
    return lax.ppermute(value, Z, [(i, count - 1 - i) for i in range(count)])


def per_device(nj, nx, nh, queries, keys, values, out_grad):
    rows, width = queries.shape
    nz = 2 * nj
    scaling = 1.0 / math.sqrt(width)
    rate = scaling * math.log2(math.e)
    smem = pl.BlockSpec(memory_space=pltpu.SMEM)
    vmem = pl.BlockSpec(memory_space=pltpu.VMEM)
    own = jnp.concatenate([queries, out_grad], axis=1)
    other = mirrored(own, nz)
    blocks = [own] + [shifted(own, "x", nx, r) for r in range(1, nx)]
    blocks += [other] + [shifted(other, "x", nx, r) for r in range(1, nx)]
    mixed = jnp.concatenate(
        [keys.reshape(-1, nh, width), values.reshape(-1, nh, width)], axis=2
    ).transpose(1, 0, 2)
    kv = lax.all_to_all(
        jnp.broadcast_to(mixed, (nj, *mixed.shape)).reshape(nj * nh, *mixed.shape[1:]),
        ("zj", "head"), 0, 0, tiled=True,
    ).reshape(nj, rows, 2 * width)
    place = [lax.axis_index(a) for a in SEQ]
    where = jnp.stack([*place, place[0] * 2 // nj]).astype(jnp.int32)
    pairs = 5 * rows * nx * rows * width
    partial, mine = pl.pallas_call(
        functools.partial(forward_kernel, rate, nx),
        out_shape=(
            jax.ShapeDtypeStruct((width, 2 * nx * rows), F32),
            jax.ShapeDtypeStruct((2, nx, 8, rows), F32),
        ),
        in_specs=[smem] + [vmem] * (2 * nx + 1),
        out_specs=(vmem, vmem),
        scratch_shapes=[pltpu.VMEM((1, 2 * nx * rows), F32)] * 2,
        compiler_params=pltpu.CompilerParams(vmem_limit_bytes=VMEM),
        cost_estimate=pl.CostEstimate(flops=4 * pairs, bytes_accessed=2 << 20, transcendentals=0),
        name="forward",
    )(where, *blocks, kv)
    groups = [[z * nx + x for z in (m, nz - 1 - m) for x in range(nx)] for m in range(nj)]
    stats = lax.all_to_all(
        jnp.broadcast_to(mine, (2 * nx, *mine.shape)), SEQ, 0, 0,
        axis_index_groups=groups, tiled=True,
    )
    *parts, dkv = pl.pallas_call(
        functools.partial(backward_kernel, rate, scaling, nx),
        out_shape=(jax.ShapeDtypeStruct((2 * rows, 2 * width), BF16),) * nx
        + (jax.ShapeDtypeStruct(kv.shape, BF16),),
        in_specs=[smem] + [vmem] * (2 * nx + 4),
        out_specs=(vmem,) * (nx + 1),
        scratch_shapes=[
            pltpu.VMEM((width, 2 * nx * rows), F32),
            pltpu.VMEM((1, 2 * nx * rows), F32),
            pltpu.VMEM((1, 2 * nx * rows), F32),
            pltpu.VMEM(kv.shape, F32),
        ],
        compiler_params=pltpu.CompilerParams(vmem_limit_bytes=VMEM),
        cost_estimate=pl.CostEstimate(flops=10 * pairs, bytes_accessed=2 << 20, transcendentals=0),
        name="backward",
    )(where, *blocks, kv, partial, mine, stats)
    arrived = [shifted(parts[-r % nx], "x", nx, r) for r in range(1, nx)]
    total = functools.reduce(jnp.add, [a.astype(F32) for a in [parts[0], *arrived]])
    back = mirrored(total[rows:].astype(BF16), nz)
    dkv = lax.all_to_all(dkv, "zj", 0, 0, tiled=True)
    dkv = jnp.sum(dkv.astype(F32), axis=0)
    total = total[:rows] + back.astype(F32)
    return total[:, width:].astype(BF16), total[:, :width], dkv[:, :width], dkv[:, width:]


def solution(mesh):
    nh = mesh.shape["head"]
    split = Mesh(mesh.devices.reshape(4, 2, -1, nh), (*SEQ, "head"))
    return jax.shard_map(
        functools.partial(per_device, 4, split.shape["x"], nh),
        mesh=split,
        in_specs=(P(SEQ, "head"), P((*SEQ, "head"), None), P((*SEQ, "head"), None), P(SEQ, "head")),
        out_specs=(P(SEQ, "head"),) * 4,
        check_vma=False,
    )
```

time: 115 us -> 111 us (0.965)
  Pallas kernels: 7.89 us -> 14.8 us
  waiting for transfers between devices: 45.2 us -> 39.5 us
  local copies, waits for them, and re-layouts: 6.62 us -> 4.73 us
  blocking collectives: 19.5 us -> 17.7 us
  starting transfers between devices: 33.3 us -> 31.7 us
    all_to_all x2, waiting for transfers between devices: 33.7 us -> 0.01 us  [the longest x1 0.01 us: per_device(): lax.all_to_all(jnp.broadcast_to(mixed, (nj, *mixed.shape)).reshape(nj * n...]
    ppermute x0 -> x2, waiting for transfers between devices: none -> 24.5 us  [mirrored(): return lax.ppermute(value, Z, [(i, count - 1 - i) for i in range(count)])]
    all_to_all x2, starting transfers between devices: 25.2 us -> 15.6 us  [the longest x1 11.8 us: per_device(): lax.all_to_all(jnp.broadcast_to(mixed, (nj, *mixed.shape)).reshape(nj * n...]
    ppermute x6 -> x9, starting transfers between devices: 8.11 us -> 12.8 us  [shifted(): lax.ppermute(value, axis, [(i, (i + step) % count) for i in range(count)])]
    pallas_call x1, Pallas kernels: 3.68 us -> 7.26 us  [per_device(): pl.pallas_call(functools.partial(forward_kernel, rate, nx), out_shape=(ja...]
    ppermute x6 -> x9, waiting for transfers between devices: 11.5 us -> 15 us  [shifted(): lax.ppermute(value, axis, [(i, (i + step) % count) for i in range(count)])]
    ppermute x0 -> x2, starting transfers between devices: none -> 3.37 us  [mirrored(): return lax.ppermute(value, Z, [(i, count - 1 - i) for i in range(count)])]
    pallas_call x1, Pallas kernels: 4.22 us -> 7.51 us  [per_device(): pl.pallas_call(functools.partial(backward_kernel, rate, scaling, nx), out...]
  transfers between devices with their start and end apart: 8 -> 13, of which waited for: 7 -> 7; matrix products, arithmetic and copies ran while one was open for 2% -> 1% of each run, Pallas kernels for 0% -> 0%
where the time goes in v2:
time: 111 us; the launch traced here: 110 us
  waiting for transfers between devices  39.5 us (36%)
  starting transfers between devices  31.7 us (29%)
  blocking collectives  17.7 us (16%)
  Pallas kernels  14.8 us (13%)
  local copies, waits for them, and re-layouts  4.73 us (4%)
    ppermute x2, waiting for transfers between devices, mirrored(): return lax.ppermute(value, Z, [(i, count - 1 - i) for i in range(count)])  24.5 us
    all_to_all x1, blocking collectives, per_device(): lax.all_to_all(jnp.broadcast_to(mine, (2 * nx, *mine.shape)), SEQ, 0, 0,...  17.7 us
    ppermute x9, waiting for transfers between devices, shifted(): lax.ppermute(value, axis, [(i, (i + step) % count) for i in range(count)])  15 us
    ppermute x9, starting transfers between devices, shifted(): lax.ppermute(value, axis, [(i, (i + step) % count) for i in range(count)])  12.8 us
    all_to_all x1, starting transfers between devices, per_device(): lax.all_to_all(jnp.broadcast_to(mixed, (nj, *mixed.shape)).reshape(nj * n...  11.8 us
    pallas_call x1, Pallas kernels, per_device(): pl.pallas_call(functools.partial(backward_kernel, rate, scaling, nx), out...  7.51 us
    pallas_call x1, Pallas kernels, per_device(): pl.pallas_call(functools.partial(forward_kernel, rate, nx), out_shape=(ja...  7.26 us
    all_to_all x1, starting transfers between devices, per_device(): dkv = lax.all_to_all(dkv, 'zj', 0, 0, tiled=True)  3.75 us
  transfers between devices with their start and end apart: 13, of which 7 were waited for; matrix products, arithmetic and copies ran while one was open for 1% of the time, Pallas kernels for 0%

profile of v2, /device:TPU:8, one launch (start us, length us, event | category | flops | bytes accessed | tf_op | source)
XLA Modules:
  0.0 109.5 jit_solution(7215459125096610918)
XLA Ops:
  0.6 0.0 copy-start
  0.6 0.9 copy.9
  1.5 0.0 copy-done
  1.6 0.9 broadcast_in_dim.6
  2.5 0.0 copy-start.1
  2.5 11.8 %all-to-all-start = ((bf16[32,32,256]{2,1,0:T(8,128)(2,1)}), bf16[32,32,256]{2,1,0:T(8,128)(2,1)S(1)}, u32[]{:S(2)}, u32[]{:S(2)}) async-start(bf16[32,32,256]{2,1,0:T(8,128)(2,1)} %bitcast.5), calls=%async_computation | async-start | bytes 1048576 | tf_op jit(solution)/shard_map/all_to_all | solution.py:173
  14.3 0.0 copy-done.1
  14.3 0.0 copy-start.2
  14.4 0.8 copy-done.2
  15.2 3.3 %collective-permute-start.3 = (bf16[256,256]{1,0:T(8,128)(2,1)S(1)}, bf16[256,256]{1,0:T(8,128)(2,1)S(1)}, u32[]{:S(2)}, u32[]{:S(2)}) collective-permute-start(bf16[256,256]{1,0:T(8,128)(2,1)S(1)} %constant_dynamic-update-slice_fusion.refs_0_), channel_id=1, source_target_pairs={{0,224},{32,192},{64,160},{96,128},{128,96},{160,64},{192,32},{224... | collective-permute-start | bytes 393224 | tf_op jit(solution)/shard_map/ppermute | solution.py:156
  18.5 2.8 %collective-permute-start.2 = (bf16[256,256]{1,0:T(8,128)(2,1)S(1)}, bf16[256,256]{1,0:T(8,128)(2,1)S(1)}, u32[]{:S(2)}, u32[]{:S(2)}) collective-permute-start(bf16[256,256]{1,0:T(8,128)(2,1)S(1)} %constant_dynamic-update-slice_fusion.refs_0_), channel_id=1, source_target_pairs={{0,24},{8,0},{16,8},{24,16},{1,25},{9,1},{17,9},{25,17},{2,26},{10... | collective-permute-start | bytes 393224 | tf_op jit(solution)/shard_map/ppermute | solution.py:152
  21.2 0.8 collective-permute-start.1
  22.0 0.9 collective-permute-start
  22.9 12.5 %collective-permute-done.3.refs_4_ = bf16[256,256]{1,0:T(8,128)(2,1)S(1)} collective-permute-done((bf16[256,256]{1,0:T(8,128)(2,1)S(1)}, bf16[256,256]{1,0:T(8,128)(2,1)S(1)}, u32[]{:S(2)}, u32[]{:S(2)}) %collective-permute-start.3) | collective-permute-done | bytes 131104 | tf_op jit(solution)/shard_map/ppermute | solution.py:156
  35.4 2.8 %collective-permute-start.6 = (bf16[256,256]{1,0:T(8,128)(2,1)S(1)}, bf16[256,256]{1,0:T(8,128)(2,1)S(1)}, u32[]{:S(2)}, u32[]{:S(2)}) collective-permute-start(bf16[256,256]{1,0:T(8,128)(2,1)S(1)} %collective-permute-done.3.refs_4_), channel_id=1, source_target_pairs={{0,24},{8,0},{16,8},{24,16},{1,25},{9,1},{17,9},{25,17},{2,26},{10... | collective-permute-start | bytes 393224 | tf_op jit(solution)/shard_map/ppermute | solution.py:152
  38.2 0.8 collective-permute-start.5
  39.0 0.0 collective-permute-done.2.refs_3_
  39.0 0.9 collective-permute-start.4
  39.9 0.1 pad_add_fusion.where_ref
  40.0 0.0 collective-permute-done.1.refs_2_
  40.0 0.0 collective-permute-done.refs_1_
  40.0 3.6 %collective-permute-done.6.refs_7_ = bf16[256,256]{1,0:T(8,128)(2,1)S(1)} collective-permute-done((bf16[256,256]{1,0:T(8,128)(2,1)S(1)}, bf16[256,256]{1,0:T(8,128)(2,1)S(1)}, u32[]{:S(2)}, u32[]{:S(2)}) %collective-permute-start.6) | collective-permute-done | bytes 131104 | tf_op jit(solution)/shard_map/ppermute | solution.py:152
  43.5 2.3 %collective-permute-done.5.refs_6_ = bf16[256,256]{1,0:T(8,128)(2,1)S(1)} collective-permute-done((bf16[256,256]{1,0:T(8,128)(2,1)S(1)}, bf16[256,256]{1,0:T(8,128)(2,1)S(1)}, u32[]{:S(2)}, u32[]{:S(2)}) %collective-permute-start.5) | collective-permute-done | bytes 131104 | tf_op jit(solution)/shard_map/ppermute | solution.py:152
  45.8 1.4 %collective-permute-done.4.refs_5_ = bf16[256,256]{1,0:T(8,128)(2,1)S(1)} collective-permute-done((bf16[256,256]{1,0:T(8,128)(2,1)S(1)}, bf16[256,256]{1,0:T(8,128)(2,1)S(1)}, u32[]{:S(2)}, u32[]{:S(2)}) %collective-permute-start.4) | collective-permute-done | bytes 131104 | tf_op jit(solution)/shard_map/ppermute | solution.py:152
  47.2 0.0 all-to-all-done
  47.2 7.3 %forward.1 = (f32[128,2048]{1,0:T(8,128)S(1)}, f32[2,4,8,256]{3,2,1,0:T(8,128)S(1)}) custom-call(s32[4]{0:T(128)S(1)} %pad_add_fusion.where_ref, bf16[256,256]{1,0:T(8,128)(2,1)S(1)} %constant_dynamic-update-slice_fusion.refs_0_, bf16[256,256]{1,0:T(8,128)(2,1)S(1)} %collective-permute-done.refs_1_, bf16[256,256]{1,0:T(8,128)(2,1)S(1)} %collective-permute-done.1.refs_2_, ...), custom_call_target="tpu_custom_call" | custom-call | flops 671088640 | bytes 2097152 | tf_op jit(solution)/shard_map/forward/pallas_call | solution.py:180
  54.5 17.7 %all_to_all.15.refs_11_ = f32[8,2,4,8,256]{4,3,2,1,0:T(8,128)S(1)} all-to-all(f32[8,2,4,8,256]{4,3,2,1,0:T(8,128)S(1)} %broadcast_in_dim.7), channel_id=1, replica_groups={{0,8,16,24,224,232,240,248},{32,40,48,56,192,200,208,216},{64,72,80,88,..., dimensions={0} | all-to-all | bytes 1048576 | tf_op jit(solution)/shard_map/all_to_all | solution.py:194
  72.2 7.5 %backward.1 = (bf16[512,256]{1,0:T(8,128)(2,1)S(1)}, bf16[512,256]{1,0:T(8,128)(2,1)S(1)}, bf16[512,256]{1,0:T(8,128)(2,1)S(1)}, bf16[512,256]{1,0:T(8,128)(2,1)S(1)}, bf16[4,256,256]{2,1,0:T(8,128)(2,1)}) custom-call(s32[4]{0:T(128)S(1)} %pad_add_fusion.where_ref, bf16[256,256]{1,0:T(8,128)(2,1)S(1)} %constant_dynamic-update-slice_fusion.refs_0_, ...), custom_call_target="tpu_custom_call" | custom-call | flops 1677721600 | bytes 2097152 | tf_op jit(solution)/shard_map/backward/pallas_call | solution.py:198
  79.7 0.0 collective-permute-start.7
  79.7 2.4 %collective-permute-start.8 = (bf16[512,256]{1,0:T(8,128)(2,1)S(1)}, bf16[512,256]{1,0:T(8,128)(2,1)S(1)}, u32[]{:S(2)}, u32[]{:S(2)}) collective-permute-start(bf16[512,256]{1,0:T(8,128)(2,1)S(1)} %get-tuple-element.15), channel_id=1, source_target_pairs={{0,16},{8,24},{16,0},{24,8},{1,17},{9,25},{17,1},{25,9},{2,18},{10... | collective-permute-start | bytes 786440 | tf_op jit(solution)/shard_map/ppermute | solution.py:152
  82.2 1.5 %collective-permute-start.9 = (bf16[512,256]{1,0:T(8,128)(2,1)S(1)}, bf16[512,256]{1,0:T(8,128)(2,1)S(1)}, u32[]{:S(2)}, u32[]{:S(2)}) collective-permute-start(bf16[512,256]{1,0:T(8,128)(2,1)S(1)} %get-tuple-element.16), channel_id=1, source_target_pairs={{0,24},{8,0},{16,8},{24,16},{1,25},{9,1},{17,9},{25,17},{2,26},{10... | collective-permute-start | bytes 786440 | tf_op jit(solution)/shard_map/ppermute | solution.py:152
  83.6 3.7 %all-to-all-start.2 = ((bf16[4,256,256]{2,1,0:T(8,128)(2,1)}), bf16[4,256,256]{2,1,0:T(8,128)(2,1)S(1)}, u32[]{:S(2)}, u32[]{:S(2)}) async-start(bf16[4,256,256]{2,1,0:T(8,128)(2,1)} %get-tuple-element.17), calls=%async_computation.2 | async-start | bytes 1048576 | tf_op jit(solution)/shard_map/all_to_all | solution.py:217
  87.4 7.1 %collective-permute-done.7 = bf16[512,256]{1,0:T(8,128)(2,1)S(1)} collective-permute-done((bf16[512,256]{1,0:T(8,128)(2,1)S(1)}, bf16[512,256]{1,0:T(8,128)(2,1)S(1)}, u32[]{:S(2)}, u32[]{:S(2)}) %collective-permute-start.7) | collective-permute-done | bytes 262176 | tf_op jit(solution)/shard_map/ppermute | solution.py:152
  94.5 0.0 collective-permute-done.8
  94.5 0.6 collective-permute-done.9
  95.1 0.1 convert_add_fusion
  95.3 0.1 collective-permute-start.10
  95.4 12.0 %collective-permute-done.10 = bf16[256,256]{1,0:T(8,128)(2,1)S(1)} collective-permute-done((bf16[256,256]{1,0:T(8,128)(2,1)S(1)}, bf16[256,256]{1,0:T(8,128)(2,1)S(1)}, u32[]{:S(2)}, u32[]{:S(2)}) %collective-permute-start.10) | collective-permute-done | bytes 131104 | tf_op jit(solution)/shard_map/ppermute | solution.py:156
  107.4 0.6 slice.36
  108.1 0.7 slice.29
  108.7 0.0 all-to-all-done.2
  108.7 0.1 convert_reduce_fusion
  108.8 0.7 fusion
  (8 shorter events, 0.2 us)
Async XLA Ops:
  0.6 0.9 copy-start
  2.5 11.8 %copy-start.1 = (bf16[256,128]{1,0:T(8,128)(2,1)S(1)}, bf16[256,128]{1,0:T(8,128)(2,1)}, u32[]{:S(2)}) copy-start(bf16[256,128]{1,0:T(8,128)(2,1)} %param.4) | copy-start | bytes 196612
  2.5 44.7 %all-to-all-start = ((bf16[32,32,256]{2,1,0:T(8,128)(2,1)}), bf16[32,32,256]{2,1,0:T(8,128)(2,1)S(1)}, u32[]{:S(2)}, u32[]{:S(2)}) async-start(bf16[32,32,256]{2,1,0:T(8,128)(2,1)} %bitcast.5), calls=%async_computation | async-start | bytes 1048576 | tf_op jit(solution)/shard_map/all_to_all | solution.py:173
  14.3 0.8 copy-start.2
  15.2 20.2 %collective-permute-start.3 = (bf16[256,256]{1,0:T(8,128)(2,1)S(1)}, bf16[256,256]{1,0:T(8,128)(2,1)S(1)}, u32[]{:S(2)}, u32[]{:S(2)}) collective-permute-start(bf16[256,256]{1,0:T(8,128)(2,1)S(1)} %constant_dynamic-update-slice_fusion.refs_0_), channel_id=1, source_target_pairs={{0,224},{32,192},{64,160},{96,128},{128,96},{160,64},{192,32},{224... | collective-permute-start | bytes 393224 | tf_op jit(solution)/shard_map/ppermute | solution.py:156
  18.5 20.5 %collective-permute-start.2 = (bf16[256,256]{1,0:T(8,128)(2,1)S(1)}, bf16[256,256]{1,0:T(8,128)(2,1)S(1)}, u32[]{:S(2)}, u32[]{:S(2)}) collective-permute-start(bf16[256,256]{1,0:T(8,128)(2,1)S(1)} %constant_dynamic-update-slice_fusion.refs_0_), channel_id=1, source_target_pairs={{0,24},{8,0},{16,8},{24,16},{1,25},{9,1},{17,9},{25,17},{2,26},{10... | collective-permute-start | bytes 393224 | tf_op jit(solution)/shard_map/ppermute | solution.py:152
  21.2 18.7 %collective-permute-start.1 = (bf16[256,256]{1,0:T(8,128)(2,1)S(1)}, bf16[256,256]{1,0:T(8,128)(2,1)S(1)}, u32[]{:S(2)}, u32[]{:S(2)}) collective-permute-start(bf16[256,256]{1,0:T(8,128)(2,1)S(1)} %constant_dynamic-update-slice_fusion.refs_0_), channel_id=1, source_target_pairs={{0,16},{8,24},{16,0},{24,8},{1,17},{9,25},{17,1},{25,9},{2,18},{10... | collective-permute-start | bytes 393224 | tf_op jit(solution)/shard_map/ppermute | solution.py:152
  22.0 17.9 %collective-permute-start = (bf16[256,256]{1,0:T(8,128)(2,1)S(1)}, bf16[256,256]{1,0:T(8,128)(2,1)S(1)}, u32[]{:S(2)}, u32[]{:S(2)}) collective-permute-start(bf16[256,256]{1,0:T(8,128)(2,1)S(1)} %constant_dynamic-update-slice_fusion.refs_0_), channel_id=1, source_target_pairs={{0,8},{8,16},{16,24},{24,0},{1,9},{9,17},{17,25},{25,1},{2,10},{10... | collective-permute-start | bytes 393224 | tf_op jit(solution)/shard_map/ppermute | solution.py:152
  35.4 8.1 %collective-permute-start.6 = (bf16[256,256]{1,0:T(8,128)(2,1)S(1)}, bf16[256,256]{1,0:T(8,128)(2,1)S(1)}, u32[]{:S(2)}, u32[]{:S(2)}) collective-permute-start(bf16[256,256]{1,0:T(8,128)(2,1)S(1)} %collective-permute-done.3.refs_4_), channel_id=1, source_target_pairs={{0,24},{8,0},{16,8},{24,16},{1,25},{9,1},{17,9},{25,17},{2,26},{10... | collective-permute-start | bytes 393224 | tf_op jit(solution)/shard_map/ppermute | solution.py:152
  38.2 7.6 %collective-permute-start.5 = (bf16[256,256]{1,0:T(8,128)(2,1)S(1)}, bf16[256,256]{1,0:T(8,128)(2,1)S(1)}, u32[]{:S(2)}, u32[]{:S(2)}) collective-permute-start(bf16[256,256]{1,0:T(8,128)(2,1)S(1)} %collective-permute-done.3.refs_4_), channel_id=1, source_target_pairs={{0,16},{8,24},{16,0},{24,8},{1,17},{9,25},{17,1},{25,9},{2,18},{10... | collective-permute-start | bytes 393224 | tf_op jit(solution)/shard_map/ppermute | solution.py:152
  39.0 8.2 %collective-permute-start.4 = (bf16[256,256]{1,0:T(8,128)(2,1)S(1)}, bf16[256,256]{1,0:T(8,128)(2,1)S(1)}, u32[]{:S(2)}, u32[]{:S(2)}) collective-permute-start(bf16[256,256]{1,0:T(8,128)(2,1)S(1)} %collective-permute-done.3.refs_4_), channel_id=1, source_target_pairs={{0,8},{8,16},{16,24},{24,0},{1,9},{9,17},{17,25},{25,1},{2,10},{10... | collective-permute-start | bytes 393224 | tf_op jit(solution)/shard_map/ppermute | solution.py:152
  79.7 14.8 %collective-permute-start.7 = (bf16[512,256]{1,0:T(8,128)(2,1)S(1)}, bf16[512,256]{1,0:T(8,128)(2,1)S(1)}, u32[]{:S(2)}, u32[]{:S(2)}) collective-permute-start(bf16[512,256]{1,0:T(8,128)(2,1)S(1)} %get-tuple-element.14), channel_id=1, source_target_pairs={{0,8},{8,16},{16,24},{24,0},{1,9},{9,17},{17,25},{25,1},{2,10},{10... | collective-permute-start | bytes 786440 | tf_op jit(solution)/shard_map/ppermute | solution.py:152
  79.7 14.8 %collective-permute-start.8 = (bf16[512,256]{1,0:T(8,128)(2,1)S(1)}, bf16[512,256]{1,0:T(8,128)(2,1)S(1)}, u32[]{:S(2)}, u32[]{:S(2)}) collective-permute-start(bf16[512,256]{1,0:T(8,128)(2,1)S(1)} %get-tuple-element.15), channel_id=1, source_target_pairs={{0,16},{8,24},{16,0},{24,8},{1,17},{9,25},{17,1},{25,9},{2,18},{10... | collective-permute-start | bytes 786440 | tf_op jit(solution)/shard_map/ppermute | solution.py:152
  82.2 13.0 %collective-permute-start.9 = (bf16[512,256]{1,0:T(8,128)(2,1)S(1)}, bf16[512,256]{1,0:T(8,128)(2,1)S(1)}, u32[]{:S(2)}, u32[]{:S(2)}) collective-permute-start(bf16[512,256]{1,0:T(8,128)(2,1)S(1)} %get-tuple-element.16), channel_id=1, source_target_pairs={{0,24},{8,0},{16,8},{24,16},{1,25},{9,1},{17,9},{25,17},{2,26},{10... | collective-permute-start | bytes 786440 | tf_op jit(solution)/shard_map/ppermute | solution.py:152
  83.6 25.1 %all-to-all-start.2 = ((bf16[4,256,256]{2,1,0:T(8,128)(2,1)}), bf16[4,256,256]{2,1,0:T(8,128)(2,1)S(1)}, u32[]{:S(2)}, u32[]{:S(2)}) async-start(bf16[4,256,256]{2,1,0:T(8,128)(2,1)} %get-tuple-element.17), calls=%async_computation.2 | async-start | bytes 1048576 | tf_op jit(solution)/shard_map/all_to_all | solution.py:217
  95.3 12.1 %collective-permute-start.10 = (bf16[256,256]{1,0:T(8,128)(2,1)S(1)}, bf16[256,256]{1,0:T(8,128)(2,1)S(1)}, u32[]{:S(2)}, u32[]{:S(2)}) collective-permute-start(bf16[256,256]{1,0:T(8,128)(2,1)S(1)} %slice.35), channel_id=1, source_target_pairs={{0,224},{32,192},{64,160},{96,128},{128,96},{160,64},{192,32},{224... | collective-permute-start | bytes 393224 | tf_op jit(solution)/shard_map/ppermute | solution.py:156

commit v3 on v2

--- a/solution.py
+++ b/solution.py
@@ -78,10 +78,10 @@
         cols = slice(at * rows, (at + 1) * rows)
         grads = jnp.transpose(q_refs[at][:, width:].astype(F32))
         to = lax.rem(x - r + nx, nx)
-        end = side ^ high
-        stat_ref[end, to, 0:1, :] = m_ref[:, cols] * rate
-        stat_ref[end, to, 1:2, :] = l_ref[:, cols]
-        stat_ref[end, to, 2:3, :] = jnp.sum(grads * o_ref[:, cols], axis=0, keepdims=True)
+        row = pl.ds((side ^ high) * nx + to, 1)
+        stat_ref[0, row, :] = m_ref[:, cols] * rate
+        stat_ref[1, row, :] = l_ref[:, cols]
+        stat_ref[2, row, :] = jnp.sum(grads * o_ref[:, cols], axis=0, keepdims=True)
 
 
 def backward_kernel(rate, scaling, nx, where_ref, *refs):
@@ -97,15 +97,15 @@
         side, r = divmod(at, nx)
         cols = slice(at * rows, (at + 1) * rows)
         here = lax.rem(x - r + nx, nx)
-        end = side ^ high
-        maxima = [stat_ref[i, end, here, 0:1, :] for i in range(n)]
+        row = pl.ds((side ^ high) * nx + here, 1)
+        maxima = [stat_ref[i, 0, row, :] for i in range(n)]
         top = functools.reduce(jnp.maximum, maxima)
         shares = [jnp.exp2(m - top) for m in maxima]
-        total = sum(stat_ref[i, end, here, 1:2, :] * w for i, w in enumerate(shares))
-        delta = sum(stat_ref[i, end, here, 2:3, :] * w for i, w in enumerate(shares))
+        total = sum(stat_ref[i, 1, row, :] * w for i, w in enumerate(shares))
+        delta = sum(stat_ref[i, 2, row, :] * w for i, w in enumerate(shares))
         norm_ref[:, cols] = top + jnp.log2(total)
         delta_ref[:, cols] = delta / total
-        share = jnp.exp2(mine_ref[end, here, 0:1, :] - top) / total
+        share = jnp.exp2(mine_ref[0, row, :] - top) / total
         out_refs[r][side * rows : (side + 1) * rows, width:] = jnp.transpose(
             o_ref[:, cols] * share
         ).astype(BF16)
@@ -170,10 +170,9 @@
     mixed = jnp.concatenate(
         [keys.reshape(-1, nh, width), values.reshape(-1, nh, width)], axis=2
     ).transpose(1, 0, 2)
-    kv = lax.all_to_all(
-        jnp.broadcast_to(mixed, (nj, *mixed.shape)).reshape(nj * nh, *mixed.shape[1:]),
-        ("zj", "head"), 0, 0, tiled=True,
-    ).reshape(nj, rows, 2 * width)
+    mixed = jnp.broadcast_to(mixed, (nj, *mixed.shape)).reshape(nj * nh, *mixed.shape[1:])
+    kv = lax.all_to_all(mixed, ("zj", "head"), 0, 0, tiled=True)
+    kv = kv.reshape(nj, rows, 2 * width)
     place = [lax.axis_index(a) for a in SEQ]
     where = jnp.stack([*place, place[0] * 2 // nj]).astype(jnp.int32)
     pairs = 5 * rows * nx * rows * width
@@ -181,7 +180,7 @@
         functools.partial(forward_kernel, rate, nx),
         out_shape=(
             jax.ShapeDtypeStruct((width, 2 * nx * rows), F32),
-            jax.ShapeDtypeStruct((2, nx, 8, rows), F32),
+            jax.ShapeDtypeStruct((3, 2 * nx, rows), F32),
         ),
         in_specs=[smem] + [vmem] * (2 * nx + 1),
         out_specs=(vmem, vmem),

time: 111 us -> 104 us (0.937)
  blocking collectives: 17.7 us -> 11.3 us
    all_to_all x1, blocking collectives: 17.7 us -> 11.3 us  [per_device(): lax.all_to_all(jnp.broadcast_to(mine, (2 * nx, *mine.shape)), SEQ, 0, 0,...]
    ppermute x9, waiting for transfers between devices: 15 us -> 13.5 us  [shifted(): lax.ppermute(value, axis, [(i, (i + step) % count) for i in range(count)])]
  transfers between devices with their start and end apart: 13 -> 13, of which waited for: 7 -> 8; matrix products, arithmetic and copies ran while one was open for 1% -> 2% of each run, Pallas kernels for 0% -> 0%
where the time goes in v3:
time: 104 us; the launch traced here: 102 us
  waiting for transfers between devices  39 us (38%)
  starting transfers between devices  31.7 us (30%)
  Pallas kernels  14.8 us (14%)
  blocking collectives  11.3 us (11%)
  local copies, waits for them, and re-layouts  4.69 us (5%)
    ppermute x2, waiting for transfers between devices, mirrored(): return lax.ppermute(value, Z, [(i, count - 1 - i) for i in range(count)])  25.4 us
    ppermute x9, waiting for transfers between devices, shifted(): lax.ppermute(value, axis, [(i, (i + step) % count) for i in range(count)])  13.5 us
    ppermute x9, starting transfers between devices, shifted(): lax.ppermute(value, axis, [(i, (i + step) % count) for i in range(count)])  12.4 us
    all_to_all x1, starting transfers between devices, per_device(): kv = lax.all_to_all(mixed, ('zj', 'head'), 0, 0, tiled=True)  11.8 us
    all_to_all x1, blocking collectives, per_device(): lax.all_to_all(jnp.broadcast_to(mine, (2 * nx, *mine.shape)), SEQ, 0, 0,...  11.3 us
    pallas_call x1, Pallas kernels, per_device(): pl.pallas_call(functools.partial(backward_kernel, rate, scaling, nx), out...  7.53 us
    pallas_call x1, Pallas kernels, per_device(): pl.pallas_call(functools.partial(forward_kernel, rate, nx), out_shape=(ja...  7.27 us
    ppermute x2, starting transfers between devices, mirrored(): return lax.ppermute(value, Z, [(i, count - 1 - i) for i in range(count)])  3.91 us
  transfers between devices with their start and end apart: 13, of which 8 were waited for; matrix products, arithmetic and copies ran while one was open for 2% of the time, Pallas kernels for 0%

profile of v3, /device:TPU:8, one launch (start us, length us, event | category | flops | bytes accessed | tf_op | source)
XLA Modules:
  0.0 102.5 jit_solution(561893039054864128)
XLA Ops:
  0.6 0.0 copy-start
  0.6 0.9 copy.9
  1.5 0.0 copy-done
  1.6 0.9 broadcast_in_dim.6
  2.5 0.0 copy-start.1
  2.5 11.8 %all-to-all-start = ((bf16[32,32,256]{2,1,0:T(8,128)(2,1)}), bf16[32,32,256]{2,1,0:T(8,128)(2,1)S(1)}, u32[]{:S(2)}, u32[]{:S(2)}) async-start(bf16[32,32,256]{2,1,0:T(8,128)(2,1)} %bitcast.5), calls=%async_computation | async-start | bytes 1048576 | tf_op jit(solution)/shard_map/all_to_all | solution.py:174
  14.3 0.0 copy-done.1
  14.3 0.0 copy-start.2
  14.4 0.8 copy-done.2
  15.2 3.3 %collective-permute-start.3 = (bf16[256,256]{1,0:T(8,128)(2,1)S(1)}, bf16[256,256]{1,0:T(8,128)(2,1)S(1)}, u32[]{:S(2)}, u32[]{:S(2)}) collective-permute-start(bf16[256,256]{1,0:T(8,128)(2,1)S(1)} %constant_dynamic-update-slice_fusion.refs_0_), channel_id=1, source_target_pairs={{0,224},{32,192},{64,160},{96,128},{128,96},{160,64},{192,32},{224... | collective-permute-start | bytes 393224 | tf_op jit(solution)/shard_map/ppermute | solution.py:156
  18.5 2.8 %collective-permute-start.2 = (bf16[256,256]{1,0:T(8,128)(2,1)S(1)}, bf16[256,256]{1,0:T(8,128)(2,1)S(1)}, u32[]{:S(2)}, u32[]{:S(2)}) collective-permute-start(bf16[256,256]{1,0:T(8,128)(2,1)S(1)} %constant_dynamic-update-slice_fusion.refs_0_), channel_id=1, source_target_pairs={{0,24},{8,0},{16,8},{24,16},{1,25},{9,1},{17,9},{25,17},{2,26},{10... | collective-permute-start | bytes 393224 | tf_op jit(solution)/shard_map/ppermute | solution.py:152
  21.2 0.8 collective-permute-start.1
  22.0 0.9 collective-permute-start
  22.9 12.5 %collective-permute-done.3.refs_4_ = bf16[256,256]{1,0:T(8,128)(2,1)S(1)} collective-permute-done((bf16[256,256]{1,0:T(8,128)(2,1)S(1)}, bf16[256,256]{1,0:T(8,128)(2,1)S(1)}, u32[]{:S(2)}, u32[]{:S(2)}) %collective-permute-start.3) | collective-permute-done | bytes 131104 | tf_op jit(solution)/shard_map/ppermute | solution.py:156
  35.4 2.8 %collective-permute-start.6 = (bf16[256,256]{1,0:T(8,128)(2,1)S(1)}, bf16[256,256]{1,0:T(8,128)(2,1)S(1)}, u32[]{:S(2)}, u32[]{:S(2)}) collective-permute-start(bf16[256,256]{1,0:T(8,128)(2,1)S(1)} %collective-permute-done.3.refs_4_), channel_id=1, source_target_pairs={{0,24},{8,0},{16,8},{24,16},{1,25},{9,1},{17,9},{25,17},{2,26},{10... | collective-permute-start | bytes 393224 | tf_op jit(solution)/shard_map/ppermute | solution.py:152
  38.2 0.8 collective-permute-start.5
  39.0 0.0 collective-permute-done.2.refs_3_
  39.0 0.9 collective-permute-start.4
  39.9 0.1 pad_add_fusion.where_ref
  40.0 0.0 collective-permute-done.1.refs_2_
  40.0 0.0 collective-permute-done.refs_1_
  40.0 3.6 %collective-permute-done.6.refs_7_ = bf16[256,256]{1,0:T(8,128)(2,1)S(1)} collective-permute-done((bf16[256,256]{1,0:T(8,128)(2,1)S(1)}, bf16[256,256]{1,0:T(8,128)(2,1)S(1)}, u32[]{:S(2)}, u32[]{:S(2)}) %collective-permute-start.6) | collective-permute-done | bytes 131104 | tf_op jit(solution)/shard_map/ppermute | solution.py:152
  43.5 2.3 %collective-permute-done.5.refs_6_ = bf16[256,256]{1,0:T(8,128)(2,1)S(1)} collective-permute-done((bf16[256,256]{1,0:T(8,128)(2,1)S(1)}, bf16[256,256]{1,0:T(8,128)(2,1)S(1)}, u32[]{:S(2)}, u32[]{:S(2)}) %collective-permute-start.5) | collective-permute-done | bytes 131104 | tf_op jit(solution)/shard_map/ppermute | solution.py:152
  45.8 1.4 %collective-permute-done.4.refs_5_ = bf16[256,256]{1,0:T(8,128)(2,1)S(1)} collective-permute-done((bf16[256,256]{1,0:T(8,128)(2,1)S(1)}, bf16[256,256]{1,0:T(8,128)(2,1)S(1)}, u32[]{:S(2)}, u32[]{:S(2)}) %collective-permute-start.4) | collective-permute-done | bytes 131104 | tf_op jit(solution)/shard_map/ppermute | solution.py:152
  47.2 0.0 all-to-all-done
  47.2 7.3 %forward.1 = (f32[128,2048]{1,0:T(8,128)S(1)}, f32[3,8,256]{2,1,0:T(8,128)S(1)}) custom-call(s32[4]{0:T(128)S(1)} %pad_add_fusion.where_ref, bf16[256,256]{1,0:T(8,128)(2,1)S(1)} %constant_dynamic-update-slice_fusion.refs_0_, bf16[256,256]{1,0:T(8,128)(2,1)S(1)} %collective-permute-done.refs_1_, bf16[256,256]{1,0:T(8,128)(2,1)S(1)} %collective-permute-done.1.refs_2_, ...), custom_call_target="tpu_custom_call" | custom-call | flops 671088640 | bytes 2097152 | tf_op jit(solution)/shard_map/forward/pallas_call | solution.py:179
  54.5 11.3 %all_to_all.15.refs_11_ = f32[8,3,8,256]{3,2,1,0:T(8,128)S(1)} all-to-all(f32[8,3,8,256]{3,2,1,0:T(8,128)S(1)} %broadcast_in_dim.7), channel_id=1, replica_groups={{0,8,16,24,224,232,240,248},{32,40,48,56,192,200,208,216},{64,72,80,88,..., dimensions={0} | all-to-all | bytes 393216 | tf_op jit(solution)/shard_map/all_to_all | solution.py:193
  65.8 7.5 %backward.1 = (bf16[512,256]{1,0:T(8,128)(2,1)S(1)}, bf16[512,256]{1,0:T(8,128)(2,1)S(1)}, bf16[512,256]{1,0:T(8,128)(2,1)S(1)}, bf16[512,256]{1,0:T(8,128)(2,1)S(1)}, bf16[4,256,256]{2,1,0:T(8,128)(2,1)}) custom-call(s32[4]{0:T(128)S(1)} %pad_add_fusion.where_ref, bf16[256,256]{1,0:T(8,128)(2,1)S(1)} %constant_dynamic-update-slice_fusion.refs_0_, ...), custom_call_target="tpu_custom_call" | custom-call | flops 1677721600 | bytes 2097152 | tf_op jit(solution)/shard_map/backward/pallas_call | solution.py:197
  73.3 0.3 collective-permute-start.7
  73.6 2.1 %collective-permute-start.8 = (bf16[512,256]{1,0:T(8,128)(2,1)S(1)}, bf16[512,256]{1,0:T(8,128)(2,1)S(1)}, u32[]{:S(2)}, u32[]{:S(2)}) collective-permute-start(bf16[512,256]{1,0:T(8,128)(2,1)S(1)} %get-tuple-element.15), channel_id=1, source_target_pairs={{0,16},{8,24},{16,0},{24,8},{1,17},{9,25},{17,1},{25,9},{2,18},{10... | collective-permute-start | bytes 786440 | tf_op jit(solution)/shard_map/ppermute | solution.py:152
  75.7 1.1 %collective-permute-start.9 = (bf16[512,256]{1,0:T(8,128)(2,1)S(1)}, bf16[512,256]{1,0:T(8,128)(2,1)S(1)}, u32[]{:S(2)}, u32[]{:S(2)}) collective-permute-start(bf16[512,256]{1,0:T(8,128)(2,1)S(1)} %get-tuple-element.16), channel_id=1, source_target_pairs={{0,24},{8,0},{16,8},{24,16},{1,25},{9,1},{17,9},{25,17},{2,26},{10... | collective-permute-start | bytes 786440 | tf_op jit(solution)/shard_map/ppermute | solution.py:152
  76.8 3.6 %all-to-all-start.2 = ((bf16[4,256,256]{2,1,0:T(8,128)(2,1)}), bf16[4,256,256]{2,1,0:T(8,128)(2,1)S(1)}, u32[]{:S(2)}, u32[]{:S(2)}) async-start(bf16[4,256,256]{2,1,0:T(8,128)(2,1)} %get-tuple-element.17), calls=%async_computation.2 | async-start | bytes 1048576 | tf_op jit(solution)/shard_map/all_to_all | solution.py:216
  80.3 2.6 %collective-permute-done.7 = bf16[512,256]{1,0:T(8,128)(2,1)S(1)} collective-permute-done((bf16[512,256]{1,0:T(8,128)(2,1)S(1)}, bf16[512,256]{1,0:T(8,128)(2,1)S(1)}, u32[]{:S(2)}, u32[]{:S(2)}) %collective-permute-start.7) | collective-permute-done | bytes 262176 | tf_op jit(solution)/shard_map/ppermute | solution.py:152
  82.9 3.6 %collective-permute-done.8 = bf16[512,256]{1,0:T(8,128)(2,1)S(1)} collective-permute-done((bf16[512,256]{1,0:T(8,128)(2,1)S(1)}, bf16[512,256]{1,0:T(8,128)(2,1)S(1)}, u32[]{:S(2)}, u32[]{:S(2)}) %collective-permute-start.8) | collective-permute-done | bytes 262176 | tf_op jit(solution)/shard_map/ppermute | solution.py:152
  86.5 0.1 collective-permute-done.9
  86.6 0.1 convert_add_fusion
  86.8 0.6 collective-permute-start.10
  87.4 12.9 %collective-permute-done.10 = bf16[256,256]{1,0:T(8,128)(2,1)S(1)} collective-permute-done((bf16[256,256]{1,0:T(8,128)(2,1)S(1)}, bf16[256,256]{1,0:T(8,128)(2,1)S(1)}, u32[]{:S(2)}, u32[]{:S(2)}) %collective-permute-start.10) | collective-permute-done | bytes 131104 | tf_op jit(solution)/shard_map/ppermute | solution.py:156
  100.4 0.6 slice.36
  101.0 0.7 slice.29
  101.7 0.0 all-to-all-done.2
  101.7 0.1 convert_reduce_fusion
  101.8 0.7 fusion
  (8 shorter events, 0.1 us)
Async XLA Ops:
  0.6 0.9 copy-start
  2.5 11.8 %copy-start.1 = (bf16[256,128]{1,0:T(8,128)(2,1)S(1)}, bf16[256,128]{1,0:T(8,128)(2,1)}, u32[]{:S(2)}) copy-start(bf16[256,128]{1,0:T(8,128)(2,1)} %param.4) | copy-start | bytes 196612
  2.5 44.7 %all-to-all-start = ((bf16[32,32,256]{2,1,0:T(8,128)(2,1)}), bf16[32,32,256]{2,1,0:T(8,128)(2,1)S(1)}, u32[]{:S(2)}, u32[]{:S(2)}) async-start(bf16[32,32,256]{2,1,0:T(8,128)(2,1)} %bitcast.5), calls=%async_computation | async-start | bytes 1048576 | tf_op jit(solution)/shard_map/all_to_all | solution.py:174
  14.3 0.8 copy-start.2
  15.2 20.2 %collective-permute-start.3 = (bf16[256,256]{1,0:T(8,128)(2,1)S(1)}, bf16[256,256]{1,0:T(8,128)(2,1)S(1)}, u32[]{:S(2)}, u32[]{:S(2)}) collective-permute-start(bf16[256,256]{1,0:T(8,128)(2,1)S(1)} %constant_dynamic-update-slice_fusion.refs_0_), channel_id=1, source_target_pairs={{0,224},{32,192},{64,160},{96,128},{128,96},{160,64},{192,32},{224... | collective-permute-start | bytes 393224 | tf_op jit(solution)/shard_map/ppermute | solution.py:156
  18.5 20.5 %collective-permute-start.2 = (bf16[256,256]{1,0:T(8,128)(2,1)S(1)}, bf16[256,256]{1,0:T(8,128)(2,1)S(1)}, u32[]{:S(2)}, u32[]{:S(2)}) collective-permute-start(bf16[256,256]{1,0:T(8,128)(2,1)S(1)} %constant_dynamic-update-slice_fusion.refs_0_), channel_id=1, source_target_pairs={{0,24},{8,0},{16,8},{24,16},{1,25},{9,1},{17,9},{25,17},{2,26},{10... | collective-permute-start | bytes 393224 | tf_op jit(solution)/shard_map/ppermute | solution.py:152
  21.2 18.7 %collective-permute-start.1 = (bf16[256,256]{1,0:T(8,128)(2,1)S(1)}, bf16[256,256]{1,0:T(8,128)(2,1)S(1)}, u32[]{:S(2)}, u32[]{:S(2)}) collective-permute-start(bf16[256,256]{1,0:T(8,128)(2,1)S(1)} %constant_dynamic-update-slice_fusion.refs_0_), channel_id=1, source_target_pairs={{0,16},{8,24},{16,0},{24,8},{1,17},{9,25},{17,1},{25,9},{2,18},{10... | collective-permute-start | bytes 393224 | tf_op jit(solution)/shard_map/ppermute | solution.py:152
  22.0 17.9 %collective-permute-start = (bf16[256,256]{1,0:T(8,128)(2,1)S(1)}, bf16[256,256]{1,0:T(8,128)(2,1)S(1)}, u32[]{:S(2)}, u32[]{:S(2)}) collective-permute-start(bf16[256,256]{1,0:T(8,128)(2,1)S(1)} %constant_dynamic-update-slice_fusion.refs_0_), channel_id=1, source_target_pairs={{0,8},{8,16},{16,24},{24,0},{1,9},{9,17},{17,25},{25,1},{2,10},{10... | collective-permute-start | bytes 393224 | tf_op jit(solution)/shard_map/ppermute | solution.py:152
  35.4 8.1 %collective-permute-start.6 = (bf16[256,256]{1,0:T(8,128)(2,1)S(1)}, bf16[256,256]{1,0:T(8,128)(2,1)S(1)}, u32[]{:S(2)}, u32[]{:S(2)}) collective-permute-start(bf16[256,256]{1,0:T(8,128)(2,1)S(1)} %collective-permute-done.3.refs_4_), channel_id=1, source_target_pairs={{0,24},{8,0},{16,8},{24,16},{1,25},{9,1},{17,9},{25,17},{2,26},{10... | collective-permute-start | bytes 393224 | tf_op jit(solution)/shard_map/ppermute | solution.py:152
  38.2 7.6 %collective-permute-start.5 = (bf16[256,256]{1,0:T(8,128)(2,1)S(1)}, bf16[256,256]{1,0:T(8,128)(2,1)S(1)}, u32[]{:S(2)}, u32[]{:S(2)}) collective-permute-start(bf16[256,256]{1,0:T(8,128)(2,1)S(1)} %collective-permute-done.3.refs_4_), channel_id=1, source_target_pairs={{0,16},{8,24},{16,0},{24,8},{1,17},{9,25},{17,1},{25,9},{2,18},{10... | collective-permute-start | bytes 393224 | tf_op jit(solution)/shard_map/ppermute | solution.py:152
  39.0 8.2 %collective-permute-start.4 = (bf16[256,256]{1,0:T(8,128)(2,1)S(1)}, bf16[256,256]{1,0:T(8,128)(2,1)S(1)}, u32[]{:S(2)}, u32[]{:S(2)}) collective-permute-start(bf16[256,256]{1,0:T(8,128)(2,1)S(1)} %collective-permute-done.3.refs_4_), channel_id=1, source_target_pairs={{0,8},{8,16},{16,24},{24,0},{1,9},{9,17},{17,25},{25,1},{2,10},{10... | collective-permute-start | bytes 393224 | tf_op jit(solution)/shard_map/ppermute | solution.py:152
  73.3 9.6 %collective-permute-start.7 = (bf16[512,256]{1,0:T(8,128)(2,1)S(1)}, bf16[512,256]{1,0:T(8,128)(2,1)S(1)}, u32[]{:S(2)}, u32[]{:S(2)}) collective-permute-start(bf16[512,256]{1,0:T(8,128)(2,1)S(1)} %get-tuple-element.14), channel_id=1, source_target_pairs={{0,8},{8,16},{16,24},{24,0},{1,9},{9,17},{17,25},{25,1},{2,10},{10... | collective-permute-start | bytes 786440 | tf_op jit(solution)/shard_map/ppermute | solution.py:152
  73.6 12.9 %collective-permute-start.8 = (bf16[512,256]{1,0:T(8,128)(2,1)S(1)}, bf16[512,256]{1,0:T(8,128)(2,1)S(1)}, u32[]{:S(2)}, u32[]{:S(2)}) collective-permute-start(bf16[512,256]{1,0:T(8,128)(2,1)S(1)} %get-tuple-element.15), channel_id=1, source_target_pairs={{0,16},{8,24},{16,0},{24,8},{1,17},{9,25},{17,1},{25,9},{2,18},{10... | collective-permute-start | bytes 786440 | tf_op jit(solution)/shard_map/ppermute | solution.py:152
  75.7 10.9 %collective-permute-start.9 = (bf16[512,256]{1,0:T(8,128)(2,1)S(1)}, bf16[512,256]{1,0:T(8,128)(2,1)S(1)}, u32[]{:S(2)}, u32[]{:S(2)}) collective-permute-start(bf16[512,256]{1,0:T(8,128)(2,1)S(1)} %get-tuple-element.16), channel_id=1, source_target_pairs={{0,24},{8,0},{16,8},{24,16},{1,25},{9,1},{17,9},{25,17},{2,26},{10... | collective-permute-start | bytes 786440 | tf_op jit(solution)/shard_map/ppermute | solution.py:152
  76.8 24.9 %all-to-all-start.2 = ((bf16[4,256,256]{2,1,0:T(8,128)(2,1)}), bf16[4,256,256]{2,1,0:T(8,128)(2,1)S(1)}, u32[]{:S(2)}, u32[]{:S(2)}) async-start(bf16[4,256,256]{2,1,0:T(8,128)(2,1)} %get-tuple-element.17), calls=%async_computation.2 | async-start | bytes 1048576 | tf_op jit(solution)/shard_map/all_to_all | solution.py:216
  86.8 13.6 %collective-permute-start.10 = (bf16[256,256]{1,0:T(8,128)(2,1)S(1)}, bf16[256,256]{1,0:T(8,128)(2,1)S(1)}, u32[]{:S(2)}, u32[]{:S(2)}) collective-permute-start(bf16[256,256]{1,0:T(8,128)(2,1)S(1)} %slice.35), channel_id=1, source_target_pairs={{0,224},{32,192},{64,160},{96,128},{128,96},{160,64},{192,32},{224... | collective-permute-start | bytes 393224 | tf_op jit(solution)/shard_map/ppermute | solution.py:156
